TPU v7x, 128 devices: a 2x2x16 block of a 8x8x16 slice. The times are simulated.
128 devices in a mesh: kpt: 4 (over x, y), gx: 32 (over z, core).
Axes of the slice: x: 2, y: 2, z: 16, core: 2. Of those that a mesh axis runs over, the one named last changes fastest.
The devices are a block of a 8x8x16 slice.
Arguments:
- e_field: float32 [2, 3, 256, 512, 128], P(None, None, ('kpt', 'gx')), parts along dimension 2, may hold values from -6 to 6
- h_field: float32 [2, 3, 256, 512, 128], P(None, None, ('kpt', 'gx')), parts along dimension 2, may hold values from -6 to 6
- labels: int32 [256, 512, 128], P(('kpt', 'gx')), parts along dimension 0, may hold values from 0 to 3
- kpoint: int32 [8], P('kpt'), parts along dimension 0, may hold values from 0 to 15
- eps_inf: float32 [4], replicated, may hold values from 1 to 12
- delta_eps: float32 [4], replicated, may hold values from 0.5 to 4
- omega_zero: float32 [4], replicated, may hold values from 0.2 to 1
- damping: float32 [4], replicated, may hold values from 0.05 to 0.8
Outputs:
- e_final: float32 [2, 3, 256, 512, 128], P(None, None, ('kpt', 'gx')), parts along dimension 2
- h_final: float32 [2, 3, 256, 512, 128], P(None, None, ('kpt', 'gx')), parts along dimension 2
There are 4 independent parts, one for each index of `kpt`. A program takes and returns all parts, laid end to end along the dimension named above; an argument that names none is the same for every part. Nothing has to cross between parts.
Inputs may be any that keep to these rules, and one draw needn't show every extreme that they name: `kpoint`: entry 0 indexes the k-point along x, entry 1 along y, out of 16 each.
All inputs are finite; a program needn't handle non-finite values.
Results may differ from a plain program's by a relative error of at most 0.00002.
Values sent between devices are 32-bit elements; how exact they have to be, the bound alone decides.
A program may use at most 128 MiB of HBM per device.

v0:
```python
import math

import jax
import jax.numpy as jnp
from jax import lax
from jax.sharding import PartitionSpec as P

ITERS = 12
KGRID = 16


time_step = 0.5


def shifted(value, axis, by):
    size = lax.axis_size(axis)
    return lax.ppermute(value, axis, [(i, (i + by) % size) for i in range(size)])


def cmul(field, cosv, sinv):
    return jnp.stack([field[0] * cosv - field[1] * sinv, field[0] * sinv + field[1] * cosv])


def next_y(field, cosv, sinv):
    rolled = jnp.roll(field, -1, axis=-2)
    last = cmul(rolled[..., -1:, :], cosv, sinv)
    return jnp.concatenate([rolled[..., :-1, :], last], axis=-2)


def prev_y(field, cosv, sinv):
    rolled = jnp.roll(field, 1, axis=-2)
    first = cmul(rolled[..., :1, :], cosv, -sinv)
    return jnp.concatenate([first, rolled[..., 1:, :]], axis=-2)


def next_z(field):
    zeros = jnp.zeros(field.shape[:-1] + (1,), jnp.float32)
    return jnp.concatenate([field[..., 1:], zeros], axis=-1)


def prev_z(field):
    zeros = jnp.zeros(field.shape[:-1] + (1,), jnp.float32)
    return jnp.concatenate([zeros, field[..., :-1]], axis=-1)


def per_cell(labels, table):
    picked = jnp.zeros(labels.shape, jnp.float32)
    for label in range(table.shape[0]):
        picked = picked + jnp.where(labels == label, table[label], jnp.float32(0.0))
    return picked


def update_magnetic(efield, hfield, right_ey, right_ez, cos_y, sin_y):
    ex, ey, ez = (efield[:, 0], efield[:, 1], efield[:, 2])
    next_ey = jnp.concatenate([ey[:, 1:], right_ey], axis=1)
    next_ez = jnp.concatenate([ez[:, 1:], right_ez], axis=1)
    curl_x = next_y(ez, cos_y, sin_y) - ez - (next_z(ey) - ey)
    curl_y = next_z(ex) - ex - (next_ez - ez)
    curl_z = next_ey - ey - (next_y(ex, cos_y, sin_y) - ex)
    return hfield - time_step * jnp.stack([curl_x, curl_y, curl_z], axis=1)


def update_electric(efield, hfield, polar, current, left_hy, left_hz, coeffs, cos_y, sin_y):
    ce, ja, jb, de = coeffs
    hx, hy, hz = (hfield[:, 0], hfield[:, 1], hfield[:, 2])
    prev_hy = jnp.concatenate([left_hy, hy[:, :-1]], axis=1)
    prev_hz = jnp.concatenate([left_hz, hz[:, :-1]], axis=1)
    kurl_x = hz - prev_y(hz, cos_y, sin_y) - (hy - prev_z(hy))
    kurl_y = hx - prev_z(hx) - (hz - prev_hz)
    kurl_z = hy - prev_hy - (hx - prev_y(hx, cos_y, sin_y))
    kurl = jnp.stack([kurl_x, kurl_y, kurl_z], axis=1)
    current = ja * current + jb * (de * efield - polar)
    polar = polar + time_step * current
    efield = efield + ce * (kurl - current)
    return (efield, polar, current)


def shards(e_field, h_field, labels, kpoint, eps_inf, delta_eps, omega_zero, damping):
    theta_x = jnp.float32(2.0 * math.pi) * kpoint[0].astype(jnp.float32) / KGRID
    theta_y = jnp.float32(2.0 * math.pi) * kpoint[1].astype(jnp.float32) / KGRID
    cos_x, sin_x = (jnp.cos(theta_x), jnp.sin(theta_x))
    cos_y, sin_y = (jnp.cos(theta_y), jnp.sin(theta_y))
    half = damping * time_step / 2.0
    coeffs = (
        per_cell(labels, time_step / eps_inf),
        per_cell(labels, (1.0 - half) / (1.0 + half)),
        per_cell(labels, time_step * omega_zero * omega_zero / (1.0 + half)),
        per_cell(labels, delta_eps),
    )
    position = lax.axis_index("gx")
    at_first = position == 0
    at_last = position == lax.axis_size("gx") - 1
    start_ghost = jnp.zeros((2, 2, 1) + h_field.shape[3:], jnp.float32)

    def advance(step, carry):
        efield, hfield, polar, current, ghost = carry
        planes = efield[:, 1:3, 0:1]
        right = shifted(planes, "gx", -1)
        right = jnp.where(at_last, cmul(right, cos_x, sin_x), right)
        new_h = update_magnetic(efield, hfield, right[:, 0], right[:, 1], cos_y, sin_y)
        hplanes = new_h[:, 1:3, -1:]
        left = shifted(hplanes, "gx", 1)
        left = jnp.where(at_first, cmul(left, cos_x, -sin_x), left)
        left_hy, left_hz = (left[:, 0], left[:, 1])
        new_e, polar, current = update_electric(
            efield, new_h, polar, current, left_hy, left_hz, coeffs, cos_y, sin_y
        )
        return (new_e, new_h, polar, current, ghost)

    zeros = jnp.zeros(e_field.shape, jnp.float32)
    efield, hfield, polar, current, ghost = lax.fori_loop(
        0, ITERS, advance, (e_field, h_field, zeros, zeros, start_ghost)
    )
    return (efield, hfield)


def solution(mesh):
    placed = (
        P(None, None, ("kpt", "gx"), None, None),
        P(None, None, ("kpt", "gx"), None, None),
        P(("kpt", "gx"), None, None),
        P("kpt"),
        P(),
        P(),
        P(),
        P(),
    )
    return jax.shard_map(
        shards,
        mesh=mesh,
        in_specs=placed,
        out_specs=(
            P(None, None, ("kpt", "gx"), None, None),
            P(None, None, ("kpt", "gx"), None, None),
        ),
        check_vma=False,
    )
```

profile of v0, /device:TPU:86, one launch (start us, length us, event | category | flops | bytes accessed | tf_op | source)
XLA Modules:
  0.0 523.6 jit_solution(4285877269049631706)
XLA Ops:
  0.6 3.8 copy.112
  9.2 4.9 select_add_fusion
  14.0 9.1 %select_add_fusion.1 = (f32[2,512,128]{2,1,0:T(8,128)}, f32[2,512,128]{2,1,0:T(8,128)}, f32[2,512,128]{2,1,0:T(8,128)}) fusion(pred[2,512,128]{2,1,0:T(8,128)(4,1)S(1)} %get-tuple-element.245, pred[2,512,128]{2,1,0:T(8,128)(4,1)S(1)} %get-tuple-element.244, pred[2,512,128]{2,1,0:T(8,128)(4,1)S(1)} %get-tuple-element.243, ...), kind=kLoop, calls=%fused_computation.64 | loop fusion | flops 2752512 | bytes 2097200 | tf_op jit(solution)/shard_map/add | solution.py:49
  23.2 498.8 %while.18 = (s32[]{:T(128)}, f32[2,3,2,512,128]{4,3,2,1,0:T(8,128)S(1)}, f32[2,3,2,512,128]{4,3,2,1,0:T(8,128)}, f32[2,3,2,512,128]{4,3,2,1,0:T(8,128)}, f32[2,3...) while((s32[]{:T(128)}, ...), condition=%wide.region_1.2_spmd.clone, body=%wide.region_0.1_spmd.clone.sunk | while | flops 24124420 | bytes 196016720 | solution.py:111
  24.4 12.0 %collective-permute-start = (f32[2,2,1,512,128]{4,3,0,2,1:T(8,128)}, f32[2,2,1,512,128]{4,3,0,2,1:T(8,128)}, u32[]{:S(2)}, u32[]{:S(2)}) collective-permute-start(f32[2,2,1,512,128]{4,3,0,2,1:T(8,128)} %slice.472), channel_id=1, source_target_pairs={{0,31},{1,0},{2,1},{3,2},{4,3},{5,4},{6,5},{7,6},{8,7},{9,8},{10,9... | collective-permute-start | bytes 3145736 | tf_op jit(solution)/shard_map/while/body/eval_jaxpr/ppermute | solution.py:17
  39.7 1.7 slice.474
  43.5 5.7 %multiply_add_fusion.7 = (f32[2,3,2,512,128]{4,3,2,1,0:T(8,128)}, f32[2,3,2,512,128]{4,3,2,1,0:T(8,128)S(1)}) fusion(f32[2,3,2,512,128]{4,3,2,1,0:T(8,128)} %get-tuple-element.473, pred[]{:T(512)S(6)} %compare.7, f32[2,3,2,512,128]{4,3,2,1,0:T(8,128)S(1)} %get-tuple-element.471, f32[2,512,128]{2,1,0:T(8,128)S(1)} %copy-done.8, ...), kind=kLoop, calls=%fused_computation.8.clone.1 | loop fusion | flops 7077888 | bytes 17301504 | tf_op jit(solution)/shard_map/while/body/eval_jaxpr/add | solution.py:73
  49.2 2.1 multiply_subtract_fusion.10
  51.3 1.4 maximum_select_fusion.2
  56.9 15.0 %collective-permute-done.1 = f32[2,2,1,512,128]{4,3,2,1,0:T(8,128)S(1)} collective-permute-done((f32[2,2,1,512,128]{4,3,2,1,0:T(8,128)S(1)}, f32[2,2,1,512,128]{4,3,2,1,0:T(8,128)S(1)}, u32[]{:S(2)}, u32[]{:S(2)}) %collective-permute-start.1) | collective-permute-done | bytes 1048608 | tf_op jit(solution)/shard_map/while/body/eval_jaxpr/ppermute | solution.py:17
  79.4 1.7 slice.474
  83.2 6.7 %multiply_add_fusion.7 = (f32[2,3,2,512,128]{4,3,2,1,0:T(8,128)}, f32[2,3,2,512,128]{4,3,2,1,0:T(8,128)S(1)}) fusion(f32[2,3,2,512,128]{4,3,2,1,0:T(8,128)} %get-tuple-element.473, pred[]{:T(512)S(6)} %compare.7, f32[2,3,2,512,128]{4,3,2,1,0:T(8,128)S(1)} %get-tuple-element.471, f32[2,512,128]{2,1,0:T(8,128)S(1)} %copy-done.8, ...), kind=kLoop, calls=%fused_computation.8.clone.1 | loop fusion | flops 7077888 | bytes 17301504 | tf_op jit(solution)/shard_map/while/body/eval_jaxpr/add | solution.py:73
  89.9 2.1 multiply_subtract_fusion.10
  91.9 1.4 maximum_select_fusion.2
  98.0 14.5 %collective-permute-done.1 = f32[2,2,1,512,128]{4,3,2,1,0:T(8,128)S(1)} collective-permute-done((f32[2,2,1,512,128]{4,3,2,1,0:T(8,128)S(1)}, f32[2,2,1,512,128]{4,3,2,1,0:T(8,128)S(1)}, u32[]{:S(2)}, u32[]{:S(2)}) %collective-permute-start.1) | collective-permute-done | bytes 1048608 | tf_op jit(solution)/shard_map/while/body/eval_jaxpr/ppermute | solution.py:17
  120.1 1.7 slice.474
  123.8 6.7 %multiply_add_fusion.7 = (f32[2,3,2,512,128]{4,3,2,1,0:T(8,128)}, f32[2,3,2,512,128]{4,3,2,1,0:T(8,128)S(1)}) fusion(f32[2,3,2,512,128]{4,3,2,1,0:T(8,128)} %get-tuple-element.473, pred[]{:T(512)S(6)} %compare.7, f32[2,3,2,512,128]{4,3,2,1,0:T(8,128)S(1)} %get-tuple-element.471, f32[2,512,128]{2,1,0:T(8,128)S(1)} %copy-done.8, ...), kind=kLoop, calls=%fused_computation.8.clone.1 | loop fusion | flops 7077888 | bytes 17301504 | tf_op jit(solution)/shard_map/while/body/eval_jaxpr/add | solution.py:73
  130.5 2.1 multiply_subtract_fusion.10
  132.6 1.4 maximum_select_fusion.2
  138.7 14.5 %collective-permute-done.1 = f32[2,2,1,512,128]{4,3,2,1,0:T(8,128)S(1)} collective-permute-done((f32[2,2,1,512,128]{4,3,2,1,0:T(8,128)S(1)}, f32[2,2,1,512,128]{4,3,2,1,0:T(8,128)S(1)}, u32[]{:S(2)}, u32[]{:S(2)}) %collective-permute-start.1) | collective-permute-done | bytes 1048608 | tf_op jit(solution)/shard_map/while/body/eval_jaxpr/ppermute | solution.py:17
  160.7 1.7 slice.474
  164.5 6.7 %multiply_add_fusion.7 = (f32[2,3,2,512,128]{4,3,2,1,0:T(8,128)}, f32[2,3,2,512,128]{4,3,2,1,0:T(8,128)S(1)}) fusion(f32[2,3,2,512,128]{4,3,2,1,0:T(8,128)} %get-tuple-element.473, pred[]{:T(512)S(6)} %compare.7, f32[2,3,2,512,128]{4,3,2,1,0:T(8,128)S(1)} %get-tuple-element.471, f32[2,512,128]{2,1,0:T(8,128)S(1)} %copy-done.8, ...), kind=kLoop, calls=%fused_computation.8.clone.1 | loop fusion | flops 7077888 | bytes 17301504 | tf_op jit(solution)/shard_map/while/body/eval_jaxpr/add | solution.py:73
  171.1 2.1 multiply_subtract_fusion.10
  173.2 1.4 maximum_select_fusion.2
  179.3 14.5 %collective-permute-done.1 = f32[2,2,1,512,128]{4,3,2,1,0:T(8,128)S(1)} collective-permute-done((f32[2,2,1,512,128]{4,3,2,1,0:T(8,128)S(1)}, f32[2,2,1,512,128]{4,3,2,1,0:T(8,128)S(1)}, u32[]{:S(2)}, u32[]{:S(2)}) %collective-permute-start.1) | collective-permute-done | bytes 1048608 | tf_op jit(solution)/shard_map/while/body/eval_jaxpr/ppermute | solution.py:17
  201.4 1.7 slice.474
  205.1 6.7 %multiply_add_fusion.7 = (f32[2,3,2,512,128]{4,3,2,1,0:T(8,128)}, f32[2,3,2,512,128]{4,3,2,1,0:T(8,128)S(1)}) fusion(f32[2,3,2,512,128]{4,3,2,1,0:T(8,128)} %get-tuple-element.473, pred[]{:T(512)S(6)} %compare.7, f32[2,3,2,512,128]{4,3,2,1,0:T(8,128)S(1)} %get-tuple-element.471, f32[2,512,128]{2,1,0:T(8,128)S(1)} %copy-done.8, ...), kind=kLoop, calls=%fused_computation.8.clone.1 | loop fusion | flops 7077888 | bytes 17301504 | tf_op jit(solution)/shard_map/while/body/eval_jaxpr/add | solution.py:73
  211.8 2.1 multiply_subtract_fusion.10
  213.9 1.4 maximum_select_fusion.2
  220.0 14.5 %collective-permute-done.1 = f32[2,2,1,512,128]{4,3,2,1,0:T(8,128)S(1)} collective-permute-done((f32[2,2,1,512,128]{4,3,2,1,0:T(8,128)S(1)}, f32[2,2,1,512,128]{4,3,2,1,0:T(8,128)S(1)}, u32[]{:S(2)}, u32[]{:S(2)}) %collective-permute-start.1) | collective-permute-done | bytes 1048608 | tf_op jit(solution)/shard_map/while/body/eval_jaxpr/ppermute | solution.py:17
  242.0 1.7 slice.474
  245.8 6.7 %multiply_add_fusion.7 = (f32[2,3,2,512,128]{4,3,2,1,0:T(8,128)}, f32[2,3,2,512,128]{4,3,2,1,0:T(8,128)S(1)}) fusion(f32[2,3,2,512,128]{4,3,2,1,0:T(8,128)} %get-tuple-element.473, pred[]{:T(512)S(6)} %compare.7, f32[2,3,2,512,128]{4,3,2,1,0:T(8,128)S(1)} %get-tuple-element.471, f32[2,512,128]{2,1,0:T(8,128)S(1)} %copy-done.8, ...), kind=kLoop, calls=%fused_computation.8.clone.1 | loop fusion | flops 7077888 | bytes 17301504 | tf_op jit(solution)/shard_map/while/body/eval_jaxpr/add | solution.py:73
  252.4 2.1 multiply_subtract_fusion.10
  254.5 1.4 maximum_select_fusion.2
  260.6 14.5 %collective-permute-done.1 = f32[2,2,1,512,128]{4,3,2,1,0:T(8,128)S(1)} collective-permute-done((f32[2,2,1,512,128]{4,3,2,1,0:T(8,128)S(1)}, f32[2,2,1,512,128]{4,3,2,1,0:T(8,128)S(1)}, u32[]{:S(2)}, u32[]{:S(2)}) %collective-permute-start.1) | collective-permute-done | bytes 1048608 | tf_op jit(solution)/shard_map/while/body/eval_jaxpr/ppermute | solution.py:17
  282.6 1.7 slice.474
  286.4 6.7 %multiply_add_fusion.7 = (f32[2,3,2,512,128]{4,3,2,1,0:T(8,128)}, f32[2,3,2,512,128]{4,3,2,1,0:T(8,128)S(1)}) fusion(f32[2,3,2,512,128]{4,3,2,1,0:T(8,128)} %get-tuple-element.473, pred[]{:T(512)S(6)} %compare.7, f32[2,3,2,512,128]{4,3,2,1,0:T(8,128)S(1)} %get-tuple-element.471, f32[2,512,128]{2,1,0:T(8,128)S(1)} %copy-done.8, ...), kind=kLoop, calls=%fused_computation.8.clone.1 | loop fusion | flops 7077888 | bytes 17301504 | tf_op jit(solution)/shard_map/while/body/eval_jaxpr/add | solution.py:73
  293.1 2.1 multiply_subtract_fusion.10
  295.2 1.4 maximum_select_fusion.2
  301.3 14.5 %collective-permute-done.1 = f32[2,2,1,512,128]{4,3,2,1,0:T(8,128)S(1)} collective-permute-done((f32[2,2,1,512,128]{4,3,2,1,0:T(8,128)S(1)}, f32[2,2,1,512,128]{4,3,2,1,0:T(8,128)S(1)}, u32[]{:S(2)}, u32[]{:S(2)}) %collective-permute-start.1) | collective-permute-done | bytes 1048608 | tf_op jit(solution)/shard_map/while/body/eval_jaxpr/ppermute | solution.py:17
  323.3 1.7 slice.474
  327.1 6.7 %multiply_add_fusion.7 = (f32[2,3,2,512,128]{4,3,2,1,0:T(8,128)}, f32[2,3,2,512,128]{4,3,2,1,0:T(8,128)S(1)}) fusion(f32[2,3,2,512,128]{4,3,2,1,0:T(8,128)} %get-tuple-element.473, pred[]{:T(512)S(6)} %compare.7, f32[2,3,2,512,128]{4,3,2,1,0:T(8,128)S(1)} %get-tuple-element.471, f32[2,512,128]{2,1,0:T(8,128)S(1)} %copy-done.8, ...), kind=kLoop, calls=%fused_computation.8.clone.1 | loop fusion | flops 7077888 | bytes 17301504 | tf_op jit(solution)/shard_map/while/body/eval_jaxpr/add | solution.py:73
  333.7 2.1 multiply_subtract_fusion.10
  335.8 1.4 maximum_select_fusion.2
  341.9 14.5 %collective-permute-done.1 = f32[2,2,1,512,128]{4,3,2,1,0:T(8,128)S(1)} collective-permute-done((f32[2,2,1,512,128]{4,3,2,1,0:T(8,128)S(1)}, f32[2,2,1,512,128]{4,3,2,1,0:T(8,128)S(1)}, u32[]{:S(2)}, u32[]{:S(2)}) %collective-permute-start.1) | collective-permute-done | bytes 1048608 | tf_op jit(solution)/shard_map/while/body/eval_jaxpr/ppermute | solution.py:17
  363.9 1.7 slice.474
  367.7 6.7 %multiply_add_fusion.7 = (f32[2,3,2,512,128]{4,3,2,1,0:T(8,128)}, f32[2,3,2,512,128]{4,3,2,1,0:T(8,128)S(1)}) fusion(f32[2,3,2,512,128]{4,3,2,1,0:T(8,128)} %get-tuple-element.473, pred[]{:T(512)S(6)} %compare.7, f32[2,3,2,512,128]{4,3,2,1,0:T(8,128)S(1)} %get-tuple-element.471, f32[2,512,128]{2,1,0:T(8,128)S(1)} %copy-done.8, ...), kind=kLoop, calls=%fused_computation.8.clone.1 | loop fusion | flops 7077888 | bytes 17301504 | tf_op jit(solution)/shard_map/while/body/eval_jaxpr/add | solution.py:73
  374.4 2.1 multiply_subtract_fusion.10
  376.4 1.4 maximum_select_fusion.2
  382.5 14.5 %collective-permute-done.1 = f32[2,2,1,512,128]{4,3,2,1,0:T(8,128)S(1)} collective-permute-done((f32[2,2,1,512,128]{4,3,2,1,0:T(8,128)S(1)}, f32[2,2,1,512,128]{4,3,2,1,0:T(8,128)S(1)}, u32[]{:S(2)}, u32[]{:S(2)}) %collective-permute-start.1) | collective-permute-done | bytes 1048608 | tf_op jit(solution)/shard_map/while/body/eval_jaxpr/ppermute | solution.py:17
  404.6 1.7 slice.474
  408.3 6.7 %multiply_add_fusion.7 = (f32[2,3,2,512,128]{4,3,2,1,0:T(8,128)}, f32[2,3,2,512,128]{4,3,2,1,0:T(8,128)S(1)}) fusion(f32[2,3,2,512,128]{4,3,2,1,0:T(8,128)} %get-tuple-element.473, pred[]{:T(512)S(6)} %compare.7, f32[2,3,2,512,128]{4,3,2,1,0:T(8,128)S(1)} %get-tuple-element.471, f32[2,512,128]{2,1,0:T(8,128)S(1)} %copy-done.8, ...), kind=kLoop, calls=%fused_computation.8.clone.1 | loop fusion | flops 7077888 | bytes 17301504 | tf_op jit(solution)/shard_map/while/body/eval_jaxpr/add | solution.py:73
  415.0 2.1 multiply_subtract_fusion.10
  417.1 1.4 maximum_select_fusion.2
  423.2 14.5 %collective-permute-done.1 = f32[2,2,1,512,128]{4,3,2,1,0:T(8,128)S(1)} collective-permute-done((f32[2,2,1,512,128]{4,3,2,1,0:T(8,128)S(1)}, f32[2,2,1,512,128]{4,3,2,1,0:T(8,128)S(1)}, u32[]{:S(2)}, u32[]{:S(2)}) %collective-permute-start.1) | collective-permute-done | bytes 1048608 | tf_op jit(solution)/shard_map/while/body/eval_jaxpr/ppermute | solution.py:17
  445.2 1.7 slice.474
  449.0 6.7 %multiply_add_fusion.7 = (f32[2,3,2,512,128]{4,3,2,1,0:T(8,128)}, f32[2,3,2,512,128]{4,3,2,1,0:T(8,128)S(1)}) fusion(f32[2,3,2,512,128]{4,3,2,1,0:T(8,128)} %get-tuple-element.473, pred[]{:T(512)S(6)} %compare.7, f32[2,3,2,512,128]{4,3,2,1,0:T(8,128)S(1)} %get-tuple-element.471, f32[2,512,128]{2,1,0:T(8,128)S(1)} %copy-done.8, ...), kind=kLoop, calls=%fused_computation.8.clone.1 | loop fusion | flops 7077888 | bytes 17301504 | tf_op jit(solution)/shard_map/while/body/eval_jaxpr/add | solution.py:73
  455.6 2.1 multiply_subtract_fusion.10
  463.8 14.5 %collective-permute-done.1 = f32[2,2,1,512,128]{4,3,2,1,0:T(8,128)S(1)} collective-permute-done((f32[2,2,1,512,128]{4,3,2,1,0:T(8,128)S(1)}, f32[2,2,1,512,128]{4,3,2,1,0:T(8,128)S(1)}, u32[]{:S(2)}, u32[]{:S(2)}) %collective-permute-start.1) | collective-permute-done | bytes 1048608 | tf_op jit(solution)/shard_map/while/body/eval_jaxpr/ppermute | solution.py:17
  485.9 1.7 slice.474
  489.6 6.7 %multiply_add_fusion.7 = (f32[2,3,2,512,128]{4,3,2,1,0:T(8,128)}, f32[2,3,2,512,128]{4,3,2,1,0:T(8,128)S(1)}) fusion(f32[2,3,2,512,128]{4,3,2,1,0:T(8,128)} %get-tuple-element.473, pred[]{:T(512)S(6)} %compare.7, f32[2,3,2,512,128]{4,3,2,1,0:T(8,128)S(1)} %get-tuple-element.471, f32[2,512,128]{2,1,0:T(8,128)S(1)} %copy-done.8, ...), kind=kLoop, calls=%fused_computation.8.clone.1 | loop fusion | flops 7077888 | bytes 17301504 | tf_op jit(solution)/shard_map/while/body/eval_jaxpr/add | solution.py:73
  496.3 2.1 multiply_subtract_fusion.10
  504.5 14.5 %collective-permute-done.1 = f32[2,2,1,512,128]{4,3,2,1,0:T(8,128)S(1)} collective-permute-done((f32[2,2,1,512,128]{4,3,2,1,0:T(8,128)S(1)}, f32[2,2,1,512,128]{4,3,2,1,0:T(8,128)S(1)}, u32[]{:S(2)}, u32[]{:S(2)}) %collective-permute-start.1) | collective-permute-done | bytes 1048608 | tf_op jit(solution)/shard_map/while/body/eval_jaxpr/ppermute | solution.py:17
  522.0 1.7 copy-done
  (646 shorter events, 173.8 us)
Async XLA Ops:
  4.4 18.8 %copy-start.1 = (f32[2,3,2,512,128]{4,3,2,1,0:T(8,128)S(1)}, f32[2,3,2,512,128]{4,3,2,1,0:T(8,128)}, u32[]{:S(2)}) copy-start(f32[2,3,2,512,128]{4,3,2,1,0:T(8,128)} %param.10) | copy-start | bytes 9437188
  24.4 24.8 %collective-permute-start = (f32[2,2,1,512,128]{4,3,0,2,1:T(8,128)}, f32[2,2,1,512,128]{4,3,0,2,1:T(8,128)}, u32[]{:S(2)}, u32[]{:S(2)}) collective-permute-start(f32[2,2,1,512,128]{4,3,0,2,1:T(8,128)} %slice.472), channel_id=1, source_target_pairs={{0,31},{1,0},{2,1},{3,2},{4,3},{5,4},{6,5},{7,6},{8,7},{9,8},{10,9... | collective-permute-start | bytes 3145736 | tf_op jit(solution)/shard_map/while/body/eval_jaxpr/ppermute | solution.py:17
  39.7 3.8 copy-start.9
  49.2 24.2 %copy-start.5 = (f32[2,3,2,512,128]{4,3,2,1,0:T(8,128)}, f32[2,3,2,512,128]{4,3,2,1,0:T(8,128)S(1)}, u32[]{:S(2)}) copy-start(f32[2,3,2,512,128]{4,3,2,1,0:T(8,128)S(1)} %get-tuple-element.493) | copy-start | bytes 9437188 | tf_op jit(solution)/shard_map/while
  56.3 16.2 %copy-start.3 = (f32[2,3,2,512,128]{4,3,2,1,0:T(8,128)}, f32[2,3,2,512,128]{4,3,2,1,0:T(8,128)S(1)}, u32[]{:S(2)}) copy-start(f32[2,3,2,512,128]{4,3,2,1,0:T(8,128)S(1)} %fusion.58) | copy-start | bytes 9437188 | tf_op jit(solution)/shard_map/while
  56.4 15.5 %collective-permute-start.1 = (f32[2,2,1,512,128]{4,3,2,1,0:T(8,128)S(1)}, f32[2,2,1,512,128]{4,3,2,1,0:T(8,128)S(1)}, u32[]{:S(2)}, u32[]{:S(2)}) collective-permute-start(f32[2,2,1,512,128]{4,3,2,1,0:T(8,128)S(1)} %slice.477), channel_id=1, source_target_pairs={{0,1},{1,2},{2,3},{3,4},{4,5},{5,6},{6,7},{7,8},{8,9},{9,10},{10,1... | collective-permute-start | bytes 3145736 | tf_op jit(solution)/shard_map/while/body/eval_jaxpr/ppermute | solution.py:17
  76.2 13.7 %collective-permute-start = (f32[2,2,1,512,128]{4,3,0,2,1:T(8,128)}, f32[2,2,1,512,128]{4,3,0,2,1:T(8,128)}, u32[]{:S(2)}, u32[]{:S(2)}) collective-permute-start(f32[2,2,1,512,128]{4,3,0,2,1:T(8,128)} %slice.472), channel_id=1, source_target_pairs={{0,31},{1,0},{2,1},{3,2},{4,3},{5,4},{6,5},{7,6},{8,7},{9,8},{10,9... | collective-permute-start | bytes 3145736 | tf_op jit(solution)/shard_map/while/body/eval_jaxpr/ppermute | solution.py:17
  79.4 3.8 copy-start.9
  89.8 24.2 %copy-start.5 = (f32[2,3,2,512,128]{4,3,2,1,0:T(8,128)}, f32[2,3,2,512,128]{4,3,2,1,0:T(8,128)S(1)}, u32[]{:S(2)}) copy-start(f32[2,3,2,512,128]{4,3,2,1,0:T(8,128)S(1)} %get-tuple-element.493) | copy-start | bytes 9437188 | tf_op jit(solution)/shard_map/while
  97.0 16.2 %copy-start.3 = (f32[2,3,2,512,128]{4,3,2,1,0:T(8,128)}, f32[2,3,2,512,128]{4,3,2,1,0:T(8,128)S(1)}, u32[]{:S(2)}) copy-start(f32[2,3,2,512,128]{4,3,2,1,0:T(8,128)S(1)} %fusion.58) | copy-start | bytes 9437188 | tf_op jit(solution)/shard_map/while
  97.1 15.5 %collective-permute-start.1 = (f32[2,2,1,512,128]{4,3,2,1,0:T(8,128)S(1)}, f32[2,2,1,512,128]{4,3,2,1,0:T(8,128)S(1)}, u32[]{:S(2)}, u32[]{:S(2)}) collective-permute-start(f32[2,2,1,512,128]{4,3,2,1,0:T(8,128)S(1)} %slice.477), channel_id=1, source_target_pairs={{0,1},{1,2},{2,3},{3,4},{4,5},{5,6},{6,7},{7,8},{8,9},{9,10},{10,1... | collective-permute-start | bytes 3145736 | tf_op jit(solution)/shard_map/while/body/eval_jaxpr/ppermute | solution.py:17
  116.8 13.7 %collective-permute-start = (f32[2,2,1,512,128]{4,3,0,2,1:T(8,128)}, f32[2,2,1,512,128]{4,3,0,2,1:T(8,128)}, u32[]{:S(2)}, u32[]{:S(2)}) collective-permute-start(f32[2,2,1,512,128]{4,3,0,2,1:T(8,128)} %slice.472), channel_id=1, source_target_pairs={{0,31},{1,0},{2,1},{3,2},{4,3},{5,4},{6,5},{7,6},{8,7},{9,8},{10,9... | collective-permute-start | bytes 3145736 | tf_op jit(solution)/shard_map/while/body/eval_jaxpr/ppermute | solution.py:17
  120.1 3.8 copy-start.8
  120.1 3.8 copy-start.9
  130.5 24.2 %copy-start.5 = (f32[2,3,2,512,128]{4,3,2,1,0:T(8,128)}, f32[2,3,2,512,128]{4,3,2,1,0:T(8,128)S(1)}, u32[]{:S(2)}) copy-start(f32[2,3,2,512,128]{4,3,2,1,0:T(8,128)S(1)} %get-tuple-element.493) | copy-start | bytes 9437188 | tf_op jit(solution)/shard_map/while
  137.6 16.2 %copy-start.3 = (f32[2,3,2,512,128]{4,3,2,1,0:T(8,128)}, f32[2,3,2,512,128]{4,3,2,1,0:T(8,128)S(1)}, u32[]{:S(2)}) copy-start(f32[2,3,2,512,128]{4,3,2,1,0:T(8,128)S(1)} %fusion.58) | copy-start | bytes 9437188 | tf_op jit(solution)/shard_map/while
  137.7 15.5 %collective-permute-start.1 = (f32[2,2,1,512,128]{4,3,2,1,0:T(8,128)S(1)}, f32[2,2,1,512,128]{4,3,2,1,0:T(8,128)S(1)}, u32[]{:S(2)}, u32[]{:S(2)}) collective-permute-start(f32[2,2,1,512,128]{4,3,2,1,0:T(8,128)S(1)} %slice.477), channel_id=1, source_target_pairs={{0,1},{1,2},{2,3},{3,4},{4,5},{5,6},{6,7},{7,8},{8,9},{9,10},{10,1... | collective-permute-start | bytes 3145736 | tf_op jit(solution)/shard_map/while/body/eval_jaxpr/ppermute | solution.py:17
  157.4 13.7 %collective-permute-start = (f32[2,2,1,512,128]{4,3,0,2,1:T(8,128)}, f32[2,2,1,512,128]{4,3,0,2,1:T(8,128)}, u32[]{:S(2)}, u32[]{:S(2)}) collective-permute-start(f32[2,2,1,512,128]{4,3,0,2,1:T(8,128)} %slice.472), channel_id=1, source_target_pairs={{0,31},{1,0},{2,1},{3,2},{4,3},{5,4},{6,5},{7,6},{8,7},{9,8},{10,9... | collective-permute-start | bytes 3145736 | tf_op jit(solution)/shard_map/while/body/eval_jaxpr/ppermute | solution.py:17
  160.7 3.8 copy-start.9
  171.1 24.2 %copy-start.5 = (f32[2,3,2,512,128]{4,3,2,1,0:T(8,128)}, f32[2,3,2,512,128]{4,3,2,1,0:T(8,128)S(1)}, u32[]{:S(2)}) copy-start(f32[2,3,2,512,128]{4,3,2,1,0:T(8,128)S(1)} %get-tuple-element.493) | copy-start | bytes 9437188 | tf_op jit(solution)/shard_map/while
  178.3 16.2 %copy-start.3 = (f32[2,3,2,512,128]{4,3,2,1,0:T(8,128)}, f32[2,3,2,512,128]{4,3,2,1,0:T(8,128)S(1)}, u32[]{:S(2)}) copy-start(f32[2,3,2,512,128]{4,3,2,1,0:T(8,128)S(1)} %fusion.58) | copy-start | bytes 9437188 | tf_op jit(solution)/shard_map/while
  178.3 15.5 %collective-permute-start.1 = (f32[2,2,1,512,128]{4,3,2,1,0:T(8,128)S(1)}, f32[2,2,1,512,128]{4,3,2,1,0:T(8,128)S(1)}, u32[]{:S(2)}, u32[]{:S(2)}) collective-permute-start(f32[2,2,1,512,128]{4,3,2,1,0:T(8,128)S(1)} %slice.477), channel_id=1, source_target_pairs={{0,1},{1,2},{2,3},{3,4},{4,5},{5,6},{6,7},{7,8},{8,9},{9,10},{10,1... | collective-permute-start | bytes 3145736 | tf_op jit(solution)/shard_map/while/body/eval_jaxpr/ppermute | solution.py:17
  198.1 13.7 %collective-permute-start = (f32[2,2,1,512,128]{4,3,0,2,1:T(8,128)}, f32[2,2,1,512,128]{4,3,0,2,1:T(8,128)}, u32[]{:S(2)}, u32[]{:S(2)}) collective-permute-start(f32[2,2,1,512,128]{4,3,0,2,1:T(8,128)} %slice.472), channel_id=1, source_target_pairs={{0,31},{1,0},{2,1},{3,2},{4,3},{5,4},{6,5},{7,6},{8,7},{9,8},{10,9... | collective-permute-start | bytes 3145736 | tf_op jit(solution)/shard_map/while/body/eval_jaxpr/ppermute | solution.py:17
  201.4 3.8 copy-start.9
  211.8 24.2 %copy-start.5 = (f32[2,3,2,512,128]{4,3,2,1,0:T(8,128)}, f32[2,3,2,512,128]{4,3,2,1,0:T(8,128)S(1)}, u32[]{:S(2)}) copy-start(f32[2,3,2,512,128]{4,3,2,1,0:T(8,128)S(1)} %get-tuple-element.493) | copy-start | bytes 9437188 | tf_op jit(solution)/shard_map/while
  218.9 16.2 %copy-start.3 = (f32[2,3,2,512,128]{4,3,2,1,0:T(8,128)}, f32[2,3,2,512,128]{4,3,2,1,0:T(8,128)S(1)}, u32[]{:S(2)}) copy-start(f32[2,3,2,512,128]{4,3,2,1,0:T(8,128)S(1)} %fusion.58) | copy-start | bytes 9437188 | tf_op jit(solution)/shard_map/while
  219.0 15.5 %collective-permute-start.1 = (f32[2,2,1,512,128]{4,3,2,1,0:T(8,128)S(1)}, f32[2,2,1,512,128]{4,3,2,1,0:T(8,128)S(1)}, u32[]{:S(2)}, u32[]{:S(2)}) collective-permute-start(f32[2,2,1,512,128]{4,3,2,1,0:T(8,128)S(1)} %slice.477), channel_id=1, source_target_pairs={{0,1},{1,2},{2,3},{3,4},{4,5},{5,6},{6,7},{7,8},{8,9},{9,10},{10,1... | collective-permute-start | bytes 3145736 | tf_op jit(solution)/shard_map/while/body/eval_jaxpr/ppermute | solution.py:17
  238.7 13.7 %collective-permute-start = (f32[2,2,1,512,128]{4,3,0,2,1:T(8,128)}, f32[2,2,1,512,128]{4,3,0,2,1:T(8,128)}, u32[]{:S(2)}, u32[]{:S(2)}) collective-permute-start(f32[2,2,1,512,128]{4,3,0,2,1:T(8,128)} %slice.472), channel_id=1, source_target_pairs={{0,31},{1,0},{2,1},{3,2},{4,3},{5,4},{6,5},{7,6},{8,7},{9,8},{10,9... | collective-permute-start | bytes 3145736 | tf_op jit(solution)/shard_map/while/body/eval_jaxpr/ppermute | solution.py:17
  242.0 3.8 copy-start.8
  242.0 3.8 copy-start.9
  252.4 24.2 %copy-start.5 = (f32[2,3,2,512,128]{4,3,2,1,0:T(8,128)}, f32[2,3,2,512,128]{4,3,2,1,0:T(8,128)S(1)}, u32[]{:S(2)}) copy-start(f32[2,3,2,512,128]{4,3,2,1,0:T(8,128)S(1)} %get-tuple-element.493) | copy-start | bytes 9437188 | tf_op jit(solution)/shard_map/while
  259.5 16.2 %copy-start.3 = (f32[2,3,2,512,128]{4,3,2,1,0:T(8,128)}, f32[2,3,2,512,128]{4,3,2,1,0:T(8,128)S(1)}, u32[]{:S(2)}) copy-start(f32[2,3,2,512,128]{4,3,2,1,0:T(8,128)S(1)} %fusion.58) | copy-start | bytes 9437188 | tf_op jit(solution)/shard_map/while
  259.6 15.5 %collective-permute-start.1 = (f32[2,2,1,512,128]{4,3,2,1,0:T(8,128)S(1)}, f32[2,2,1,512,128]{4,3,2,1,0:T(8,128)S(1)}, u32[]{:S(2)}, u32[]{:S(2)}) collective-permute-start(f32[2,2,1,512,128]{4,3,2,1,0:T(8,128)S(1)} %slice.477), channel_id=1, source_target_pairs={{0,1},{1,2},{2,3},{3,4},{4,5},{5,6},{6,7},{7,8},{8,9},{9,10},{10,1... | collective-permute-start | bytes 3145736 | tf_op jit(solution)/shard_map/while/body/eval_jaxpr/ppermute | solution.py:17
  279.4 13.7 %collective-permute-start = (f32[2,2,1,512,128]{4,3,0,2,1:T(8,128)}, f32[2,2,1,512,128]{4,3,0,2,1:T(8,128)}, u32[]{:S(2)}, u32[]{:S(2)}) collective-permute-start(f32[2,2,1,512,128]{4,3,0,2,1:T(8,128)} %slice.472), channel_id=1, source_target_pairs={{0,31},{1,0},{2,1},{3,2},{4,3},{5,4},{6,5},{7,6},{8,7},{9,8},{10,9... | collective-permute-start | bytes 3145736 | tf_op jit(solution)/shard_map/while/body/eval_jaxpr/ppermute | solution.py:17
  282.6 3.8 copy-start.9
  293.1 24.2 %copy-start.5 = (f32[2,3,2,512,128]{4,3,2,1,0:T(8,128)}, f32[2,3,2,512,128]{4,3,2,1,0:T(8,128)S(1)}, u32[]{:S(2)}) copy-start(f32[2,3,2,512,128]{4,3,2,1,0:T(8,128)S(1)} %get-tuple-element.493) | copy-start | bytes 9437188 | tf_op jit(solution)/shard_map/while
  300.2 16.2 %copy-start.3 = (f32[2,3,2,512,128]{4,3,2,1,0:T(8,128)}, f32[2,3,2,512,128]{4,3,2,1,0:T(8,128)S(1)}, u32[]{:S(2)}) copy-start(f32[2,3,2,512,128]{4,3,2,1,0:T(8,128)S(1)} %fusion.58) | copy-start | bytes 9437188 | tf_op jit(solution)/shard_map/while
  300.3 15.5 %collective-permute-start.1 = (f32[2,2,1,512,128]{4,3,2,1,0:T(8,128)S(1)}, f32[2,2,1,512,128]{4,3,2,1,0:T(8,128)S(1)}, u32[]{:S(2)}, u32[]{:S(2)}) collective-permute-start(f32[2,2,1,512,128]{4,3,2,1,0:T(8,128)S(1)} %slice.477), channel_id=1, source_target_pairs={{0,1},{1,2},{2,3},{3,4},{4,5},{5,6},{6,7},{7,8},{8,9},{9,10},{10,1... | collective-permute-start | bytes 3145736 | tf_op jit(solution)/shard_map/while/body/eval_jaxpr/ppermute | solution.py:17
  320.0 13.7 %collective-permute-start = (f32[2,2,1,512,128]{4,3,0,2,1:T(8,128)}, f32[2,2,1,512,128]{4,3,0,2,1:T(8,128)}, u32[]{:S(2)}, u32[]{:S(2)}) collective-permute-start(f32[2,2,1,512,128]{4,3,0,2,1:T(8,128)} %slice.472), channel_id=1, source_target_pairs={{0,31},{1,0},{2,1},{3,2},{4,3},{5,4},{6,5},{7,6},{8,7},{9,8},{10,9... | collective-permute-start | bytes 3145736 | tf_op jit(solution)/shard_map/while/body/eval_jaxpr/ppermute | solution.py:17
  323.3 3.8 copy-start.8
  323.3 3.8 copy-start.9
  333.7 24.2 %copy-start.5 = (f32[2,3,2,512,128]{4,3,2,1,0:T(8,128)}, f32[2,3,2,512,128]{4,3,2,1,0:T(8,128)S(1)}, u32[]{:S(2)}) copy-start(f32[2,3,2,512,128]{4,3,2,1,0:T(8,128)S(1)} %get-tuple-element.493) | copy-start | bytes 9437188 | tf_op jit(solution)/shard_map/while
  340.8 16.2 %copy-start.3 = (f32[2,3,2,512,128]{4,3,2,1,0:T(8,128)}, f32[2,3,2,512,128]{4,3,2,1,0:T(8,128)S(1)}, u32[]{:S(2)}) copy-start(f32[2,3,2,512,128]{4,3,2,1,0:T(8,128)S(1)} %fusion.58) | copy-start | bytes 9437188 | tf_op jit(solution)/shard_map/while
  340.9 15.5 %collective-permute-start.1 = (f32[2,2,1,512,128]{4,3,2,1,0:T(8,128)S(1)}, f32[2,2,1,512,128]{4,3,2,1,0:T(8,128)S(1)}, u32[]{:S(2)}, u32[]{:S(2)}) collective-permute-start(f32[2,2,1,512,128]{4,3,2,1,0:T(8,128)S(1)} %slice.477), channel_id=1, source_target_pairs={{0,1},{1,2},{2,3},{3,4},{4,5},{5,6},{6,7},{7,8},{8,9},{9,10},{10,1... | collective-permute-start | bytes 3145736 | tf_op jit(solution)/shard_map/while/body/eval_jaxpr/ppermute | solution.py:17
  360.7 13.7 %collective-permute-start = (f32[2,2,1,512,128]{4,3,0,2,1:T(8,128)}, f32[2,2,1,512,128]{4,3,0,2,1:T(8,128)}, u32[]{:S(2)}, u32[]{:S(2)}) collective-permute-start(f32[2,2,1,512,128]{4,3,0,2,1:T(8,128)} %slice.472), channel_id=1, source_target_pairs={{0,31},{1,0},{2,1},{3,2},{4,3},{5,4},{6,5},{7,6},{8,7},{9,8},{10,9... | collective-permute-start | bytes 3145736 | tf_op jit(solution)/shard_map/while/body/eval_jaxpr/ppermute | solution.py:17
  363.9 3.8 copy-start.9
  374.3 24.2 %copy-start.5 = (f32[2,3,2,512,128]{4,3,2,1,0:T(8,128)}, f32[2,3,2,512,128]{4,3,2,1,0:T(8,128)S(1)}, u32[]{:S(2)}) copy-start(f32[2,3,2,512,128]{4,3,2,1,0:T(8,128)S(1)} %get-tuple-element.493) | copy-start | bytes 9437188 | tf_op jit(solution)/shard_map/while
  381.5 16.2 %copy-start.3 = (f32[2,3,2,512,128]{4,3,2,1,0:T(8,128)}, f32[2,3,2,512,128]{4,3,2,1,0:T(8,128)S(1)}, u32[]{:S(2)}) copy-start(f32[2,3,2,512,128]{4,3,2,1,0:T(8,128)S(1)} %fusion.58) | copy-start | bytes 9437188 | tf_op jit(solution)/shard_map/while
  381.6 15.5 %collective-permute-start.1 = (f32[2,2,1,512,128]{4,3,2,1,0:T(8,128)S(1)}, f32[2,2,1,512,128]{4,3,2,1,0:T(8,128)S(1)}, u32[]{:S(2)}, u32[]{:S(2)}) collective-permute-start(f32[2,2,1,512,128]{4,3,2,1,0:T(8,128)S(1)} %slice.477), channel_id=1, source_target_pairs={{0,1},{1,2},{2,3},{3,4},{4,5},{5,6},{6,7},{7,8},{8,9},{9,10},{10,1... | collective-permute-start | bytes 3145736 | tf_op jit(solution)/shard_map/while/body/eval_jaxpr/ppermute | solution.py:17
  401.3 13.7 %collective-permute-start = (f32[2,2,1,512,128]{4,3,0,2,1:T(8,128)}, f32[2,2,1,512,128]{4,3,0,2,1:T(8,128)}, u32[]{:S(2)}, u32[]{:S(2)}) collective-permute-start(f32[2,2,1,512,128]{4,3,0,2,1:T(8,128)} %slice.472), channel_id=1, source_target_pairs={{0,31},{1,0},{2,1},{3,2},{4,3},{5,4},{6,5},{7,6},{8,7},{9,8},{10,9... | collective-permute-start | bytes 3145736 | tf_op jit(solution)/shard_map/while/body/eval_jaxpr/ppermute | solution.py:17
  404.6 3.8 copy-start.9
  415.0 24.2 %copy-start.5 = (f32[2,3,2,512,128]{4,3,2,1,0:T(8,128)}, f32[2,3,2,512,128]{4,3,2,1,0:T(8,128)S(1)}, u32[]{:S(2)}) copy-start(f32[2,3,2,512,128]{4,3,2,1,0:T(8,128)S(1)} %get-tuple-element.493) | copy-start | bytes 9437188 | tf_op jit(solution)/shard_map/while
  422.1 16.2 %copy-start.3 = (f32[2,3,2,512,128]{4,3,2,1,0:T(8,128)}, f32[2,3,2,512,128]{4,3,2,1,0:T(8,128)S(1)}, u32[]{:S(2)}) copy-start(f32[2,3,2,512,128]{4,3,2,1,0:T(8,128)S(1)} %fusion.58) | copy-start | bytes 9437188 | tf_op jit(solution)/shard_map/while
  422.2 15.5 %collective-permute-start.1 = (f32[2,2,1,512,128]{4,3,2,1,0:T(8,128)S(1)}, f32[2,2,1,512,128]{4,3,2,1,0:T(8,128)S(1)}, u32[]{:S(2)}, u32[]{:S(2)}) collective-permute-start(f32[2,2,1,512,128]{4,3,2,1,0:T(8,128)S(1)} %slice.477), channel_id=1, source_target_pairs={{0,1},{1,2},{2,3},{3,4},{4,5},{5,6},{6,7},{7,8},{8,9},{9,10},{10,1... | collective-permute-start | bytes 3145736 | tf_op jit(solution)/shard_map/while/body/eval_jaxpr/ppermute | solution.py:17
  441.9 13.7 %collective-permute-start = (f32[2,2,1,512,128]{4,3,0,2,1:T(8,128)}, f32[2,2,1,512,128]{4,3,0,2,1:T(8,128)}, u32[]{:S(2)}, u32[]{:S(2)}) collective-permute-start(f32[2,2,1,512,128]{4,3,0,2,1:T(8,128)} %slice.472), channel_id=1, source_target_pairs={{0,31},{1,0},{2,1},{3,2},{4,3},{5,4},{6,5},{7,6},{8,7},{9,8},{10,9... | collective-permute-start | bytes 3145736 | tf_op jit(solution)/shard_map/while/body/eval_jaxpr/ppermute | solution.py:17
  445.2 3.8 copy-start.9
  455.6 24.2 %copy-start.5 = (f32[2,3,2,512,128]{4,3,2,1,0:T(8,128)}, f32[2,3,2,512,128]{4,3,2,1,0:T(8,128)S(1)}, u32[]{:S(2)}) copy-start(f32[2,3,2,512,128]{4,3,2,1,0:T(8,128)S(1)} %get-tuple-element.493) | copy-start | bytes 9437188 | tf_op jit(solution)/shard_map/while
  462.8 16.2 %copy-start.3 = (f32[2,3,2,512,128]{4,3,2,1,0:T(8,128)}, f32[2,3,2,512,128]{4,3,2,1,0:T(8,128)S(1)}, u32[]{:S(2)}) copy-start(f32[2,3,2,512,128]{4,3,2,1,0:T(8,128)S(1)} %fusion.58) | copy-start | bytes 9437188 | tf_op jit(solution)/shard_map/while
  462.8 15.5 %collective-permute-start.1 = (f32[2,2,1,512,128]{4,3,2,1,0:T(8,128)S(1)}, f32[2,2,1,512,128]{4,3,2,1,0:T(8,128)S(1)}, u32[]{:S(2)}, u32[]{:S(2)}) collective-permute-start(f32[2,2,1,512,128]{4,3,2,1,0:T(8,128)S(1)} %slice.477), channel_id=1, source_target_pairs={{0,1},{1,2},{2,3},{3,4},{4,5},{5,6},{6,7},{7,8},{8,9},{9,10},{10,1... | collective-permute-start | bytes 3145736 | tf_op jit(solution)/shard_map/while/body/eval_jaxpr/ppermute | solution.py:17
  482.6 13.7 %collective-permute-start = (f32[2,2,1,512,128]{4,3,0,2,1:T(8,128)}, f32[2,2,1,512,128]{4,3,0,2,1:T(8,128)}, u32[]{:S(2)}, u32[]{:S(2)}) collective-permute-start(f32[2,2,1,512,128]{4,3,0,2,1:T(8,128)} %slice.472), channel_id=1, source_target_pairs={{0,31},{1,0},{2,1},{3,2},{4,3},{5,4},{6,5},{7,6},{8,7},{9,8},{10,9... | collective-permute-start | bytes 3145736 | tf_op jit(solution)/shard_map/while/body/eval_jaxpr/ppermute | solution.py:17
  485.9 3.8 copy-start.9
  496.3 24.2 %copy-start.5 = (f32[2,3,2,512,128]{4,3,2,1,0:T(8,128)}, f32[2,3,2,512,128]{4,3,2,1,0:T(8,128)S(1)}, u32[]{:S(2)}) copy-start(f32[2,3,2,512,128]{4,3,2,1,0:T(8,128)S(1)} %get-tuple-element.493) | copy-start | bytes 9437188 | tf_op jit(solution)/shard_map/while
  503.4 16.2 %copy-start.3 = (f32[2,3,2,512,128]{4,3,2,1,0:T(8,128)}, f32[2,3,2,512,128]{4,3,2,1,0:T(8,128)S(1)}, u32[]{:S(2)}) copy-start(f32[2,3,2,512,128]{4,3,2,1,0:T(8,128)S(1)} %fusion.58) | copy-start | bytes 9437188 | tf_op jit(solution)/shard_map/while
  503.5 15.5 %collective-permute-start.1 = (f32[2,2,1,512,128]{4,3,2,1,0:T(8,128)S(1)}, f32[2,2,1,512,128]{4,3,2,1,0:T(8,128)S(1)}, u32[]{:S(2)}, u32[]{:S(2)}) collective-permute-start(f32[2,2,1,512,128]{4,3,2,1,0:T(8,128)S(1)} %slice.477), channel_id=1, source_target_pairs={{0,1},{1,2},{2,3},{3,4},{4,5},{5,6},{6,7},{7,8},{8,9},{9,10},{10,1... | collective-permute-start | bytes 3145736 | tf_op jit(solution)/shard_map/while/body/eval_jaxpr/ppermute | solution.py:17
  (75 other events, 159.8 us)
where the time goes:
time: 526 us; the launch traced here: 524 us
  other arithmetic  195 us (37%)
  waiting for transfers between devices  175 us (33%)
  local copies, waits for them, and re-layouts  131 us (25%)
  starting transfers between devices  18.2 us (3%)
    ppermute x24, waiting for transfers between devices, shifted(): lax.ppermute(value, axis, [(i, (i + by) % size) for i in range(size)])  175 us
    add x12, other arithmetic, update_electric(): polar = polar + time_step * current  78.9 us
    slice x24, local copies, waits for them, and re-layouts, next_z(): return jnp.concatenate([field[..., 1:], zeros], axis=-1)  36.6 us
    sub x60, other arithmetic, cmul(): field[0] * cosv - field[1] * sinv  35.1 us
    while x228, local copies, waits for them, and re-layouts  25.7 us
    ppermute x24, starting transfers between devices, shifted(): lax.ppermute(value, axis, [(i, (i + by) % size) for i in range(size)])  18.2 us
    select_n x12, other arithmetic, advance(): right = jnp.where(at_last, cmul(right, cos_x, sin_x), right)  17.2 us
    add x12, other arithmetic, update_electric(): efield = efield + ce * (kurl - current)  15.6 us
  transfers between devices with their start and end apart: 24, of which 12 were waited for; matrix products, arithmetic and copies ran while one was open for 32% of the time, Pallas kernels for 0%

commit v1 on v0

v1 whole, which is shorter than its diff:
```python
import functools
import math

import jax
import jax.numpy as jnp
from jax import lax
from jax.experimental import pallas as pl
from jax.experimental.pallas import tpu as pltpu
from jax.sharding import PartitionSpec as P

MESH = pl.DeviceIdType.MESH
ITERS = 12
KGRID = 16
DT = 0.5
CHUNKS = 8
LAG = 4
BLOCK = 16
PAD = 8


def next_z(field, last):
    return jnp.where(last, 0.0, pltpu.roll(field, field.shape[1] - 1, 1))


def prev_z(field, first):
    return jnp.where(first, 0.0, pltpu.roll(field, 1, 1))


def kernel(
    e_in, h_in, labels_in, kpoint, eps_inf, delta_eps, omega_zero, damping,
    e_out, h_out,
    e, h, p, cur, ce, ja, jb, de, labels, ge, gh, phase,
    load_e, load_h, load_l, send_e, recv_e, send_h, recv_h, store_e, store_h,
):
    planes, ny, nz = labels.shape
    rows = ny // CHUNKS
    last_plane = planes - 1
    size = lax.axis_size("gx")
    me = lax.axis_index("gx")
    right = lax.rem(me + 1, size)
    left = lax.rem(me + size - 1, size)

    def span(c, pad=0):
        return pl.ds(pl.multiple_of(c * rows + pad, 8), rows)

    def get_e(c):
        return pltpu.make_async_copy(
            e_in.at[:, :, :, span(c)], e.at[:, :, :, span(c)], load_e.at[c])

    def get_h(c):
        return pltpu.make_async_copy(
            h_in.at[:, :, :, span(c)], h.at[:, :, :, span(c, PAD)], load_h.at[c])

    def get_labels():
        return pltpu.make_async_copy(labels_in, labels, load_l)

    def put_e(c):
        return pltpu.make_async_copy(
            e.at[:, :, :, span(c)], e_out.at[:, :, :, span(c)], store_e.at[c])

    def put_h(c):
        return pltpu.make_async_copy(
            h.at[:, :, :, span(c, PAD)], h_out.at[:, :, :, span(c)], store_h.at[c])

    def ship_e(c, source):
        return pltpu.make_async_remote_copy(
            src_ref=source.at[:, 1:3, 0, span(c)], dst_ref=ge.at[:, :, span(c)],
            send_sem=send_e.at[c], recv_sem=recv_e.at[c],
            device_id={"gx": left}, device_id_type=MESH)

    def ship_h(c):
        return pltpu.make_async_remote_copy(
            src_ref=h.at[:, 1:3, last_plane, span(c, PAD)], dst_ref=gh.at[:, :, span(c)],
            send_sem=send_h.at[c], recv_sem=recv_h.at[c],
            device_id={"gx": right}, device_id_type=MESH)

    barrier = pltpu.get_barrier_semaphore()
    for neighbour in (left, right):
        pl.semaphore_signal(barrier, inc=1, device_id={"gx": neighbour}, device_id_type=MESH)
    for c in range(CHUNKS):
        get_e(c).start()
        get_h(c).start()
        if c == 0:
            get_labels().start()
    pl.semaphore_wait(barrier, 2)
    for c in range(CHUNKS):
        ship_e(c, e_in).start()

    tile = (8, nz)
    turn = jnp.float32(2.0 * math.pi)
    theta_x = turn * jnp.full(tile, kpoint[0], jnp.int32).astype(jnp.float32) / KGRID
    theta_y = turn * jnp.full(tile, kpoint[1], jnp.int32).astype(jnp.float32) / KGRID
    cos_x, sin_x = jnp.cos(theta_x), jnp.sin(theta_x)
    phase[0] = jnp.where(me == size - 1, cos_x, 1.0)
    phase[1] = jnp.where(me == size - 1, sin_x, 0.0)
    phase[2] = jnp.where(me == 0, cos_x, 1.0)
    phase[3] = jnp.where(me == 0, -sin_x, 0.0)
    phase[4] = jnp.cos(theta_y)
    phase[5] = jnp.sin(theta_y)

    shape = (BLOCK, nz)

    def whole(value):
        return jnp.full(shape, value, jnp.float32)

    tables = []
    for label in range(eps_inf.shape[0]):
        half = whole(damping[label]) * (DT / 2.0)
        omega = whole(omega_zero[label])
        tables.append((
            DT / whole(eps_inf[label]),
            (1.0 - half) / (1.0 + half),
            DT * omega * omega / (1.0 + half),
            whole(delta_eps[label]),
        ))
    for which in range(4):
        for label in range(len(tables)):
            phase[8 + 4 * which + label] = tables[label][which][:8]

    def clear(block, carry):
        at = pl.ds(pl.multiple_of(block * BLOCK, 8), BLOCK)
        zero = jnp.zeros(shape, jnp.float32)
        for q in range(2):
            for comp in range(3):
                for x in range(planes):
                    p[q, comp, x, at] = zero
                    cur[q, comp, x, at] = zero
        return carry

    lax.fori_loop(0, ny // BLOCK, clear, 0)

    def spread(row):
        return jnp.concatenate([phase[row]] * (BLOCK // 8), axis=0)

    get_labels().wait()

    def media(block, carry):
        at = pl.ds(pl.multiple_of(block * BLOCK, 8), BLOCK)
        for x in range(planes):
            label = labels[x, at]
            for which, dst in enumerate((ce, ja, jb, de)):
                picked = spread(8 + 4 * which)
                for k in range(1, len(tables)):
                    picked = jnp.where(label == k, spread(8 + 4 * which + k), picked)
                dst[x, at] = picked
        return carry

    lax.fori_loop(0, ny // BLOCK, media, 0)

    column = lax.broadcasted_iota(jnp.int32, shape, 1)
    is_first, is_last = column == 0, column == nz - 1

    def wrap_e():
        cy, sy = phase[4][0:1], phase[5][0:1]
        for comp in (0, 2):
            for x in range(planes):
                re, im = e[0, comp, x, 0:1], e[1, comp, x, 0:1]
                e[0, comp, x, ny:ny + 1] = re * cy - im * sy
                e[1, comp, x, ny:ny + 1] = re * sy + im * cy

    def wrap_h():
        cy, sy = phase[4][0:1], phase[5][0:1]
        bottom = PAD + ny - 1
        for comp in (0, 2):
            for x in range(planes):
                re, im = h[0, comp, x, bottom:bottom + 1], h[1, comp, x, bottom:bottom + 1]
                h[0, comp, x, PAD - 1:PAD] = re * cy + im * sy
                h[1, comp, x, PAD - 1:PAD] = im * cy - re * sy

    def turned(ghost, at, row):
        cx, sx = spread(row), spread(row + 1)
        out = []
        for comp in range(2):
            re, im = ghost[0, comp, at], ghost[1, comp, at]
            out.append((re * cx - im * sx, re * sx + im * cx))
        return out

    def magnetic(c):
        def block(b, carry):
            y = c * rows + b * BLOCK
            at = pl.ds(pl.multiple_of(y, 8), BLOCK)
            up = pl.ds(y + 1, BLOCK)
            ath = pl.ds(pl.multiple_of(y + PAD, 8), BLOCK)
            far = turned(ge, at, 0)
            for q in range(2):
                for x in range(planes):
                    ex, ey, ez = e[q, 0, x, at], e[q, 1, x, at], e[q, 2, x, at]
                    if x == last_plane:
                        ey_x, ez_x = far[0][q], far[1][q]
                    else:
                        ey_x, ez_x = e[q, 1, x + 1, at], e[q, 2, x + 1, at]
                    ex_y, ez_y = e[q, 0, x, up], e[q, 2, x, up]
                    ex_z, ey_z = next_z(ex, is_last), next_z(ey, is_last)
                    h[q, 0, x, ath] -= DT * ((ez_y - ez) - (ey_z - ey))
                    h[q, 1, x, ath] -= DT * ((ex_z - ex) - (ez_x - ez))
                    h[q, 2, x, ath] -= DT * ((ey_x - ey) - (ex_y - ex))
            return carry

        lax.fori_loop(0, rows // BLOCK, block, 0)

    def electric(c):
        def block(b, carry):
            y = c * rows + b * BLOCK
            at = pl.ds(pl.multiple_of(y, 8), BLOCK)
            ath = pl.ds(pl.multiple_of(y + PAD, 8), BLOCK)
            down = pl.ds(y + PAD - 1, BLOCK)
            far = turned(gh, at, 2)
            for x in range(planes):
                c_e, j_a, j_b, d_e = ce[x, at], ja[x, at], jb[x, at], de[x, at]
                for q in range(2):
                    hx, hy, hz = h[q, 0, x, ath], h[q, 1, x, ath], h[q, 2, x, ath]
                    if x == 0:
                        hy_x, hz_x = far[0][q], far[1][q]
                    else:
                        hy_x, hz_x = h[q, 1, x - 1, ath], h[q, 2, x - 1, ath]
                    hx_y, hz_y = h[q, 0, x, down], h[q, 2, x, down]
                    hx_z, hy_z = prev_z(hx, is_first), prev_z(hy, is_first)
                    curls = (
                        (hz - hz_y) - (hy - hy_z),
                        (hx - hx_z) - (hz - hz_x),
                        (hy - hy_x) - (hx - hx_y),
                    )
                    for comp, curl in enumerate(curls):
                        field, polar = e[q, comp, x, at], p[q, comp, x, at]
                        current = j_a * cur[q, comp, x, at] + j_b * (d_e * field - polar)
                        cur[q, comp, x, at] = current
                        p[q, comp, x, at] = polar + DT * current
                        e[q, comp, x, at] = field + c_e * (curl - current)
            return carry

        lax.fori_loop(0, rows // BLOCK, block, 0)

    total = ITERS * CHUNKS
    get_e(0).wait()
    wrap_e()

    def advance(i, carry):
        @pl.when(i < total)
        def _():
            n, j = i // CHUNKS, i % CHUNKS
            c = (n + j) % CHUNKS

            @pl.when(n == 0)
            def _():
                @pl.when(j + 1 < CHUNKS)
                def _():
                    get_e(j + 1).wait()

                get_h(j).wait()

            @pl.when(n > 0)
            def _():
                ship_h(c).wait_send()

            ship_e(c, e).wait_recv()
            magnetic(c)

            @pl.when(c == CHUNKS - 1)
            def _():
                wrap_h()

            ship_h(c).start()

            @pl.when(n == ITERS - 1)
            def _():
                put_h(c).start()

        @pl.when(i >= LAG)
        def _():
            n, j = (i - LAG) // CHUNKS, (i - LAG) % CHUNKS
            c = (n + 1 + j) % CHUNKS
            ship_h(c).wait_recv()
            ship_e(c, e).wait_send()
            electric(c)

            @pl.when(c == 0)
            def _():
                wrap_e()

            @pl.when(n < ITERS - 1)
            def _():
                ship_e(c, e).start()

            @pl.when(n == ITERS - 1)
            def _():
                put_e(c).start()

        return carry

    lax.fori_loop(0, total + LAG, advance, 0)
    for c in range(CHUNKS):
        ship_h(c).wait_send()
        put_h(c).wait()
        put_e(c).wait()


def shards(e_field, h_field, labels, kpoint, eps_inf, delta_eps, omega_zero, damping):
    planes, ny, nz = labels.shape
    fields = (2, 3, planes)
    anywhere = pl.BlockSpec(memory_space=pl.ANY)
    scalars = pl.BlockSpec(memory_space=pltpu.SMEM)

    def vmem(*shape):
        return pltpu.VMEM(shape, jnp.float32)

    def many():
        return pltpu.SemaphoreType.DMA((CHUNKS,))

    return pl.pallas_call(
        kernel,
        out_shape=(
            jax.ShapeDtypeStruct(e_field.shape, jnp.float32),
            jax.ShapeDtypeStruct(h_field.shape, jnp.float32),
        ),
        in_specs=[anywhere] * 3 + [scalars] * 5,
        out_specs=(anywhere, anywhere),
        scratch_shapes=[
            vmem(*fields, ny + PAD, nz),
            vmem(*fields, ny + PAD, nz),
            vmem(*fields, ny, nz),
            vmem(*fields, ny, nz),
            vmem(planes, ny, nz),
            vmem(planes, ny, nz),
            vmem(planes, ny, nz),
            vmem(planes, ny, nz),
            pltpu.VMEM((planes, ny, nz), jnp.int32),
            vmem(2, 2, ny, nz),
            vmem(2, 2, ny, nz),
            vmem(24, 8, nz),
            many(), many(), pltpu.SemaphoreType.DMA,
            many(), many(), many(), many(), many(), many(),
        ],
        compiler_params=pltpu.CompilerParams(
            collective_id=0, has_side_effects=True, vmem_limit_bytes=60 * 1024 * 1024,
        ),
    )(e_field, h_field, labels, kpoint, eps_inf, delta_eps, omega_zero, damping)


def solution(mesh):
    placed = (
        P(None, None, ("kpt", "gx"), None, None),
        P(None, None, ("kpt", "gx"), None, None),
        P(("kpt", "gx"), None, None),
        P("kpt"),
        P(),
        P(),
        P(),
        P(),
    )
    return jax.shard_map(
        shards,
        mesh=mesh,
        in_specs=placed,
        out_specs=(
            P(None, None, ("kpt", "gx"), None, None),
            P(None, None, ("kpt", "gx"), None, None),
        ),
        check_vma=False,
    )
```

time: 526 us -> 164 us (0.31)
  other arithmetic: 195 us -> 0 us
  waiting for transfers between devices: 175 us -> 0 us
  Pallas kernels: 0 us -> 157 us
  local copies, waits for them, and re-layouts: 131 us -> 5.57 us
  starting transfers between devices: 18.2 us -> 0 us
    ppermute x24 -> x0, waiting for transfers between devices: 175 us -> none  [shifted(): lax.ppermute(value, axis, [(i, (i + by) % size) for i in range(size)])]
    pallas_call x0 -> x1, Pallas kernels: none -> 157 us  [shards(): pl.pallas_call(kernel, out_shape=(jax.ShapeDtypeStruct(e_field.shape, jnp...]
    add x26 -> x0, other arithmetic: 109 us -> none  [the longest x12 78.9 us: update_electric(): polar = polar + time_step * current]
    slice x88 -> x0, local copies, waits for them, and re-layouts: 54.2 us -> none  [the longest x24 36.6 us: next_z(): return jnp.concatenate([field[..., 1:], zeros], axis=-1)]
    sub x84 -> x0, other arithmetic: 46.4 us -> none  [the longest x60 35.1 us: cmul(): field[0] * cosv - field[1] * sinv]
    concatenate x48 -> x0, local copies, waits for them, and re-layouts: 26.6 us -> none  [the longest x12 15.5 us: next_y(): return jnp.concatenate([rolled[..., :-1, :], last], axis=-2)]
    while x228 -> x0, local copies, waits for them, and re-layouts: 25.7 us -> none
    select_n x24 -> x0, other arithmetic: 19.2 us -> none  [the longest x12 17.2 us: advance(): right = jnp.where(at_last, cmul(right, cos_x, sin_x), right)]
  transfers between devices with their start and end apart: 24 -> 0, of which waited for: 12 -> 0; matrix products, arithmetic and copies ran while one was open for 32% -> 0% of each run, Pallas kernels for 0% -> 0%
where the time goes in v1:
time: 164 us; the launch traced here: 163 us
  Pallas kernels  157 us (96%)
  local copies, waits for them, and re-layouts  5.57 us (3%)
    pallas_call x1, Pallas kernels, shards(): pl.pallas_call(kernel, out_shape=(jax.ShapeDtypeStruct(e_field.shape, jnp...  157 us
    unnamed x4, local copies, waits for them, and re-layouts  5.57 us

profile of v1, /device:TPU:86, one launch (start us, length us, event | category | flops | bytes accessed | tf_op | source)
XLA Modules:
  0.0 163.5 jit_solution(15654903772338929549)
XLA Ops:
  0.6 157.2 %shard_map.95 = (f32[2,3,2,512,128]{4,3,2,1,0:T(8,128)}, f32[2,3,2,512,128]{4,3,2,1,0:T(8,128)}) custom-call(f32[2,3,2,512,128]{4,3,2,1,0:T(8,128)} %e_in.1, f32[2,3,2,512,128]{4,3,2,1,0:T(8,128)} %h_in.1, s32[2,512,128]{2,1,0:T(8,128)} %labels_in.1, s32[2]{0:T(128)} %kpoint.1, f32[4]{0:T(128)} %eps_inf.1, f32[4]{0:T(128)} %delta_eps.1, f32[4]{0:T(128)} %omega_zero.1, ...), custom_call_target="tpu_custom_call" | custom-call | tf_op jit(solution)/shard_map/pallas_call | solution.py:309
  157.9 0.0 copy-start
  157.9 3.9 %copy.12 = f32[2,3,2,512,128]{4,3,2,1,0:T(8,128)} copy(f32[2,3,2,512,128]{4,3,2,1,0:T(8,128)} %get-tuple-element.4) | data formatting | bytes 6291456
  161.8 0.0 copy-done
  161.8 1.7 %copy.13 = f32[2,3,2,512,128]{4,3,2,1,0:T(8,128)} copy(f32[2,3,2,512,128]{4,3,2,1,0:T(8,128)S(1)} %copy-done) | data formatting | bytes 6291456
Async XLA Ops:
  157.9 3.9 %copy-start = (f32[2,3,2,512,128]{4,3,2,1,0:T(8,128)S(1)}, f32[2,3,2,512,128]{4,3,2,1,0:T(8,128)}, u32[]{:S(2)}) copy-start(f32[2,3,2,512,128]{4,3,2,1,0:T(8,128)} %get-tuple-element.5) | copy-start | bytes 9437188

commit v2 on v1

v2 whole, which is shorter than its diff:
```python
import functools
import math

import jax
import jax.numpy as jnp
from jax import lax
from jax.experimental import pallas as pl
from jax.experimental.pallas import tpu as pltpu
from jax.sharding import PartitionSpec as P

MESH = pl.DeviceIdType.MESH
ITERS = 12
KGRID = 16
DT = 0.5
CHUNKS = 16
AHEAD = 8
BLOCK = 16
PAD = 8
KERNEL_VMEM = 57 * 1024 * 1024


def next_z(field, last):
    return jnp.where(last, 0.0, pltpu.roll(field, field.shape[1] - 1, 1))


def prev_z(field, first):
    return jnp.where(first, 0.0, pltpu.roll(field, 1, 1))


def kernel(
    e_in, h_in, labels_in, kpoint, eps_inf, delta_eps, omega_zero, damping,
    e, h,
    p, cur, ce, ja, jb, de, labels, part, ge, ga, phase,
    load_e, load_h, load_l, send_e, recv_e, send_a, recv_a,
):
    planes, ny, nz = labels.shape
    rows = ny // CHUNKS
    last_plane = planes - 1
    size = lax.axis_size("gx")
    me = lax.axis_index("gx")
    right = lax.rem(me + 1, size)
    left = lax.rem(me + size - 1, size)

    def span(c, pad=0):
        return pl.ds(pl.multiple_of(c * rows + pad, 8), rows)

    def get_e(c):
        return pltpu.make_async_copy(
            e_in.at[:, :, :, span(c)], e.at[:, :, :, span(c)], load_e.at[c])

    def get_h(c):
        return pltpu.make_async_copy(
            h_in.at[:, :, :, span(c)], h.at[:, :, :, span(c, PAD)], load_h.at[c])

    def get_labels():
        return pltpu.make_async_copy(labels_in, labels, load_l)

    def ship_e(n, c, source):
        return pltpu.make_async_remote_copy(
            src_ref=source.at[:, 1:3, 0, span(c)], dst_ref=ge.at[n % 2, :, :, span(c)],
            send_sem=send_e.at[c], recv_sem=recv_e.at[n % 2, c],
            device_id={"gx": left}, device_id_type=MESH)

    def ship_a(n, c):
        return pltpu.make_async_remote_copy(
            src_ref=part.at[:, :, span(c)], dst_ref=ga.at[n % 2, :, :, span(c)],
            send_sem=send_a.at[c], recv_sem=recv_a.at[n % 2, c],
            device_id={"gx": right}, device_id_type=MESH)

    barrier = pltpu.get_barrier_semaphore()
    for neighbour in (left, right):
        pl.semaphore_signal(barrier, inc=1, device_id={"gx": neighbour}, device_id_type=MESH)
    get_e(0).start()
    for c in range(CHUNKS):
        if c + 1 < CHUNKS:
            get_e(c + 1).start()
        get_h(c).start()
    get_labels().start()
    pl.semaphore_wait(barrier, 2)
    for c in range(CHUNKS):
        ship_e(0, c, e_in).start()

    tile = (8, nz)
    turn = jnp.float32(2.0 * math.pi)
    theta_x = turn * jnp.full(tile, kpoint[0], jnp.int32).astype(jnp.float32) / KGRID
    theta_y = turn * jnp.full(tile, kpoint[1], jnp.int32).astype(jnp.float32) / KGRID
    cos_x, sin_x = jnp.cos(theta_x), jnp.sin(theta_x)
    phase[0] = jnp.where(me == size - 1, cos_x, 1.0)
    phase[1] = jnp.where(me == size - 1, sin_x, 0.0)
    phase[2] = jnp.where(me == 0, cos_x, 1.0)
    phase[3] = jnp.where(me == 0, -sin_x, 0.0)
    phase[4] = jnp.cos(theta_y)
    phase[5] = jnp.sin(theta_y)

    def whole(value):
        return jnp.full(tile, value, jnp.float32)

    count = eps_inf.shape[0]
    for label in range(count):
        half = whole(damping[label]) * (DT / 2.0)
        omega = whole(omega_zero[label])
        phase[8 + label] = DT / whole(eps_inf[label])
        phase[8 + count + label] = (1.0 - half) / (1.0 + half)
        phase[8 + 2 * count + label] = DT * omega * omega / (1.0 + half)
        phase[8 + 3 * count + label] = whole(delta_eps[label])

    shape = (BLOCK, nz)

    def spread(row):
        return jnp.concatenate([phase[row]] * (BLOCK // 8), axis=0)

    def media(block, carry):
        at = pl.ds(pl.multiple_of(block * BLOCK, 8), BLOCK)
        zero = jnp.zeros(shape, jnp.float32)
        for x in range(planes):
            label = labels[x, at]
            for which, dst in enumerate((ce, ja, jb, de)):
                picked = spread(8 + count * which)
                for k in range(1, count):
                    picked = jnp.where(label == k, spread(8 + count * which + k), picked)
                dst[x, at] = picked
            for q in range(2):
                for comp in range(3):
                    p[q, comp, x, at] = zero
                    cur[q, comp, x, at] = zero
        return carry

    column = lax.broadcasted_iota(jnp.int32, shape, 1)
    is_first, is_last = column == 0, column == nz - 1

    def wrap_e():
        cy, sy = phase[4][0:1], phase[5][0:1]
        for comp in (0, 2):
            for x in range(planes):
                re, im = e[0, comp, x, 0:1], e[1, comp, x, 0:1]
                e[0, comp, x, ny:ny + 1] = re * cy - im * sy
                e[1, comp, x, ny:ny + 1] = re * sy + im * cy

    def wrap_h():
        cy, sy = phase[4][0:1], phase[5][0:1]
        bottom = PAD + ny - 1
        for comp in (0, 2):
            for x in range(planes):
                re, im = h[0, comp, x, bottom:bottom + 1], h[1, comp, x, bottom:bottom + 1]
                h[0, comp, x, PAD - 1:PAD] = re * cy + im * sy
                h[1, comp, x, PAD - 1:PAD] = im * cy - re * sy

    def turned(ghost, slot, at, row):
        cx, sx = spread(row), spread(row + 1)
        out = []
        for comp in range(2):
            re, im = ghost[slot, 0, comp, at], ghost[slot, 1, comp, at]
            out.append((re * cx - im * sx, re * sx + im * cx))
        return out

    def magnetic(c):
        def block(b, carry):
            y = c * rows + b * BLOCK
            at = pl.ds(pl.multiple_of(y, 8), BLOCK)
            up = pl.ds(y + 1, BLOCK)
            ath = pl.ds(pl.multiple_of(y + PAD, 8), BLOCK)
            for q in range(2):
                for x in range(planes):
                    ex, ey, ez = e[q, 0, x, at], e[q, 1, x, at], e[q, 2, x, at]
                    ex_y, ez_y = e[q, 0, x, up], e[q, 2, x, up]
                    ex_z, ey_z = next_z(ex, is_last), next_z(ey, is_last)
                    h[q, 0, x, ath] -= DT * ((ez_y - ez) - (ey_z - ey))
                    if x == last_plane:
                        hy = h[q, 1, x, ath] - DT * ((ex_z - ex) + ez)
                        hz = h[q, 2, x, ath] + DT * (ey + (ex_y - ex))
                        part[q, 0, at] = hy
                        part[q, 1, at] = hz
                        h[q, 1, x, ath] = hy
                        h[q, 2, x, ath] = hz
                    else:
                        ey_x, ez_x = e[q, 1, x + 1, at], e[q, 2, x + 1, at]
                        h[q, 1, x, ath] -= DT * ((ex_z - ex) - (ez_x - ez))
                        h[q, 2, x, ath] -= DT * ((ey_x - ey) - (ex_y - ex))
            return carry

        lax.fori_loop(0, rows // BLOCK, block, 0)

    def complete(slot, c):
        def block(b, carry):
            y = c * rows + b * BLOCK
            at = pl.ds(pl.multiple_of(y, 8), BLOCK)
            ath = pl.ds(pl.multiple_of(y + PAD, 8), BLOCK)
            far_y, far_z = turned(ge, slot, at, 0)
            for q in range(2):
                h[q, 1, last_plane, ath] += DT * far_z[q]
                h[q, 2, last_plane, ath] -= DT * far_y[q]
            return carry

        lax.fori_loop(0, rows // BLOCK, block, 0)

    def electric(slot, c):
        def block(b, carry):
            y = c * rows + b * BLOCK
            at = pl.ds(pl.multiple_of(y, 8), BLOCK)
            ath = pl.ds(pl.multiple_of(y + PAD, 8), BLOCK)
            down = pl.ds(y + PAD - 1, BLOCK)
            far = turned(ga, slot, at, 2)
            for x in range(planes):
                c_e, j_a, j_b, d_e = ce[x, at], ja[x, at], jb[x, at], de[x, at]
                for q in range(2):
                    fields = [e[q, comp, x, at] for comp in range(3)]
                    hx, hy, hz = h[q, 0, x, ath], h[q, 1, x, ath], h[q, 2, x, ath]
                    if x == 0:
                        hy_x = far[0][q] + DT * fields[2]
                        hz_x = far[1][q] - DT * fields[1]
                    else:
                        hy_x, hz_x = h[q, 1, x - 1, ath], h[q, 2, x - 1, ath]
                    hx_y, hz_y = h[q, 0, x, down], h[q, 2, x, down]
                    hx_z, hy_z = prev_z(hx, is_first), prev_z(hy, is_first)
                    curls = (
                        (hz - hz_y) - (hy - hy_z),
                        (hx - hx_z) - (hz - hz_x),
                        (hy - hy_x) - (hx - hx_y),
                    )
                    for comp, curl in enumerate(curls):
                        field, polar = fields[comp], p[q, comp, x, at]
                        current = j_a * cur[q, comp, x, at] + j_b * (d_e * field - polar)
                        cur[q, comp, x, at] = current
                        p[q, comp, x, at] = polar + DT * current
                        e[q, comp, x, at] = field + c_e * (curl - current)
            return carry

        lax.fori_loop(0, rows // BLOCK, block, 0)

    total = ITERS * CHUNKS

    def send_part(n, c):
        magnetic(c)
        ship_a(n, c).start()

    get_e(0).wait()
    wrap_e()

    def first(j, carry):
        get_e(j + 1).wait()
        get_h(j).wait()
        send_part(0, j)
        return carry

    lax.fori_loop(0, AHEAD, first, 0)
    get_labels().wait()
    lax.fori_loop(0, ny // BLOCK, media, 0)

    def advance(i, carry):
        @pl.when(i < total)
        def _():
            n, j = i // CHUNKS, i % CHUNKS
            c = (n + j) % CHUNKS
            ship_e(n, c, e).wait_recv()
            complete(n % 2, c)

            @pl.when(c == CHUNKS - 1)
            def _():
                wrap_h()

        @pl.when(i > 0)
        def _():
            n, j = (i - 1) // CHUNKS, (i - 1) % CHUNKS
            c = (n + 1 + j) % CHUNKS
            ship_a(n, c).wait_recv()
            ship_e(n, c, e).wait_send()
            electric(n % 2, c)

            @pl.when(c == 0)
            def _():
                wrap_e()

            @pl.when(n < ITERS - 1)
            def _():
                ship_e(n + 1, c, e).start()

        @pl.when(i + AHEAD < total)
        def _():
            n, j = (i + AHEAD) // CHUNKS, (i + AHEAD) % CHUNKS
            c = (n + j) % CHUNKS

            @pl.when(n == 0)
            def _():
                @pl.when(j + 1 < CHUNKS)
                def _():
                    get_e(j + 1).wait()

                get_h(j).wait()

            @pl.when(n > 0)
            def _():
                ship_a(n, c).wait_send()

            send_part(n, c)

        return carry

    lax.fori_loop(0, total + 1, advance, 0)
    for c in range(CHUNKS):
        ship_a(ITERS - 1, c).wait_send()


def deliver(e, h, e_out, h_out, sems):
    ny = e_out.shape[3]
    copies = []
    for q in range(2):
        for comp in range(3):
            copies.append(pltpu.make_async_copy(
                e.at[q, comp, :, 0:ny], e_out.at[q, comp], sems.at[0, q, comp]))
            copies.append(pltpu.make_async_copy(
                h.at[q, comp, :, PAD:PAD + ny], h_out.at[q, comp], sems.at[1, q, comp]))
    for copy in copies:
        copy.start()
    for copy in copies:
        copy.wait()


def shards(e_field, h_field, labels, kpoint, eps_inf, delta_eps, omega_zero, damping):
    planes, ny, nz = labels.shape
    fields = (2, 3, planes)
    anywhere = pl.BlockSpec(memory_space=pltpu.HBM)
    scalars = pl.BlockSpec(memory_space=pltpu.SMEM)
    near = pl.BlockSpec(memory_space=pltpu.VMEM)

    def vmem(*shape):
        return pltpu.VMEM(shape, jnp.float32)

    def many(*lead):
        return pltpu.SemaphoreType.DMA(lead + (CHUNKS,))

    e_last, h_last = pl.pallas_call(
        kernel,
        out_shape=(vmem(*fields, ny + PAD, nz), vmem(*fields, ny + PAD, nz)),
        in_specs=[anywhere] * 3 + [scalars] * 5,
        out_specs=(near, near),
        scratch_shapes=[
            vmem(*fields, ny, nz),
            vmem(*fields, ny, nz),
            vmem(planes, ny, nz),
            vmem(planes, ny, nz),
            vmem(planes, ny, nz),
            vmem(planes, ny, nz),
            pltpu.VMEM((planes, ny, nz), jnp.int32),
            vmem(2, 2, ny, nz),
            vmem(2, 2, 2, ny, nz),
            vmem(2, 2, 2, ny, nz),
            vmem(24, 8, nz),
            many(), many(), pltpu.SemaphoreType.DMA,
            many(), many(2), many(), many(2),
        ],
        compiler_params=pltpu.CompilerParams(
            collective_id=0, has_side_effects=True, vmem_limit_bytes=KERNEL_VMEM,
        ),
    )(e_field, h_field, labels, kpoint, eps_inf, delta_eps, omega_zero, damping)
    return pl.pallas_call(
        deliver,
        out_shape=(
            jax.ShapeDtypeStruct(e_field.shape, jnp.float32),
            jax.ShapeDtypeStruct(h_field.shape, jnp.float32),
        ),
        in_specs=[near, near],
        out_specs=(anywhere, anywhere),
        scratch_shapes=[pltpu.SemaphoreType.DMA((2, 2, 3))],
        compiler_params=pltpu.CompilerParams(vmem_limit_bytes=1024 * 1024),
    )(e_last, h_last)


def solution(mesh):
    placed = (
        P(None, None, ("kpt", "gx"), None, None),
        P(None, None, ("kpt", "gx"), None, None),
        P(("kpt", "gx"), None, None),
        P("kpt"),
        P(),
        P(),
        P(),
        P(),
    )
    return jax.shard_map(
        shards,
        mesh=mesh,
        in_specs=placed,
        out_specs=(
            P(None, None, ("kpt", "gx"), None, None),
            P(None, None, ("kpt", "gx"), None, None),
        ),
        check_vma=False,
    )
```

time: 164 us -> 155 us (0.945)
  local copies, waits for them, and re-layouts: 5.57 us -> 0 us
  Pallas kernels: 157 us -> 155 us
    unnamed x4 -> x0, local copies, waits for them, and re-layouts: 5.57 us -> none
    pallas_call x1 -> x2, Pallas kernels: 157 us -> 155 us  [the longest x1 152 us: shards(): pl.pallas_call(kernel, out_shape=(vmem(*fields, ny + PAD, nz), vmem(*fiel...]
where the time goes in v2:
time: 155 us
  Pallas kernels  155 us (100%)
    pallas_call x1, Pallas kernels, shards(): pl.pallas_call(kernel, out_shape=(vmem(*fields, ny + PAD, nz), vmem(*fiel...  152 us

profile of v2, /device:TPU:86, one launch (start us, length us, event | category | flops | bytes accessed | tf_op | source)
XLA Modules:
  0.0 155.2 jit_solution(868177964758326429)
XLA Ops:
  0.6 151.8 %shard_map.95 = (f32[2,3,2,520,128]{4,3,2,1,0:T(8,128)S(1)}, f32[2,3,2,520,128]{4,3,2,1,0:T(8,128)S(1)}) custom-call(f32[2,3,2,512,128]{4,3,2,1,0:T(8,128)} %e_in.1, f32[2,3,2,512,128]{4,3,2,1,0:T(8,128)} %h_in.1, s32[2,512,128]{2,1,0:T(8,128)} %labels_in.1, s32[2]{0:T(128)} %kpoint.1, f32[4]{0:T(128)} %eps_inf.1, f32[4]{0:T(128)} %delta_eps.1, ...), custom_call_target="tpu_custom_call" | custom-call | tf_op jit(solution)/shard_map/pallas_call | solution.py:331
  152.5 2.8 %shard_map.96 = (f32[2,3,2,512,128]{4,3,2,1,0:T(8,128)}, f32[2,3,2,512,128]{4,3,2,1,0:T(8,128)}) custom-call(f32[2,3,2,520,128]{4,3,2,1,0:T(8,128)S(1)} %get-tuple-element.4.e, f32[2,3,2,520,128]{4,3,2,1,0:T(8,128)S(1)} %get-tuple-element.5.h), custom_call_target="tpu_custom_call" | custom-call | tf_op jit(solution)/shard_map/pallas_call | solution.py:355

commit v3 on v2

--- a/solution.py
+++ b/solution.py
@@ -13,8 +13,9 @@
 KGRID = 16
 DT = 0.5
 CHUNKS = 16
-AHEAD = 8
-BLOCK = 16
+AHEAD = 12
+BLOCK = 32
+PIECES = 1
 PAD = 8
 KERNEL_VMEM = 57 * 1024 * 1024
 
@@ -28,12 +29,14 @@
 
 
 def kernel(
-    e_in, h_in, labels_in, kpoint, eps_inf, delta_eps, omega_zero, damping,
+    e_in, h_in, labels_in, kpoint_in, eps_inf_in, delta_eps_in, omega_zero_in, damping_in,
     e, h,
+    kpoint, eps_inf, delta_eps, omega_zero, damping, load_s,
     p, cur, ce, ja, jb, de, labels, part, ge, ga, phase,
     load_e, load_h, load_l, send_e, recv_e, send_a, recv_a,
 ):
     planes, ny, nz = labels.shape
+    count = eps_inf.shape[0]
     rows = ny // CHUNKS
     last_plane = planes - 1
     size = lax.axis_size("gx")
@@ -44,20 +47,28 @@
     def span(c, pad=0):
         return pl.ds(pl.multiple_of(c * rows + pad, 8), rows)
 
-    def get_e(c):
+    starts = [0] + [k for k in (2, 4, 8, 16, 32) if k < CHUNKS]
+    groups = list(zip(starts, starts[1:] + [CHUNKS]))
+
+    def get_e(g):
+        low, high = groups[g]
+        at = pl.ds(low * rows, (high - low) * rows)
         return pltpu.make_async_copy(
-            e_in.at[:, :, :, span(c)], e.at[:, :, :, span(c)], load_e.at[c])
-
-    def get_h(c):
+            e_in.at[:, :, :, at], e.at[:, :, :, at], load_e.at[g])
+
+    def get_h(g):
+        low, high = groups[g]
+        at = pl.ds(low * rows, (high - low) * rows)
+        ath = pl.ds(low * rows + PAD, (high - low) * rows)
         return pltpu.make_async_copy(
-            h_in.at[:, :, :, span(c)], h.at[:, :, :, span(c, PAD)], load_h.at[c])
+            h_in.at[:, :, :, at], h.at[:, :, :, ath], load_h.at[g])
 
     def get_labels():
         return pltpu.make_async_copy(labels_in, labels, load_l)
 
-    def ship_e(n, c, source):
+    def ship_e(n, c):
         return pltpu.make_async_remote_copy(
-            src_ref=source.at[:, 1:3, 0, span(c)], dst_ref=ge.at[n % 2, :, :, span(c)],
+            src_ref=e.at[:, 1:3, 0, span(c)], dst_ref=ge.at[n % 2, :, :, span(c)],
             send_sem=send_e.at[c], recv_sem=recv_e.at[n % 2, c],
             device_id={"gx": left}, device_id_type=MESH)
 
@@ -70,41 +81,44 @@
     barrier = pltpu.get_barrier_semaphore()
     for neighbour in (left, right):
         pl.semaphore_signal(barrier, inc=1, device_id={"gx": neighbour}, device_id_type=MESH)
-    get_e(0).start()
-    for c in range(CHUNKS):
-        if c + 1 < CHUNKS:
-            get_e(c + 1).start()
-        get_h(c).start()
+    for g in range(len(groups)):
+        get_e(g).start()
+        get_h(g).start()
     get_labels().start()
-    pl.semaphore_wait(barrier, 2)
-    for c in range(CHUNKS):
-        ship_e(0, c, e_in).start()
-
-    tile = (8, nz)
-    turn = jnp.float32(2.0 * math.pi)
-    theta_x = turn * jnp.full(tile, kpoint[0], jnp.int32).astype(jnp.float32) / KGRID
-    theta_y = turn * jnp.full(tile, kpoint[1], jnp.int32).astype(jnp.float32) / KGRID
-    cos_x, sin_x = jnp.cos(theta_x), jnp.sin(theta_x)
-    phase[0] = jnp.where(me == size - 1, cos_x, 1.0)
-    phase[1] = jnp.where(me == size - 1, sin_x, 0.0)
-    phase[2] = jnp.where(me == 0, cos_x, 1.0)
-    phase[3] = jnp.where(me == 0, -sin_x, 0.0)
-    phase[4] = jnp.cos(theta_y)
-    phase[5] = jnp.sin(theta_y)
-
-    def whole(value):
-        return jnp.full(tile, value, jnp.float32)
-
-    count = eps_inf.shape[0]
-    for label in range(count):
-        half = whole(damping[label]) * (DT / 2.0)
-        omega = whole(omega_zero[label])
-        phase[8 + label] = DT / whole(eps_inf[label])
-        phase[8 + count + label] = (1.0 - half) / (1.0 + half)
-        phase[8 + 2 * count + label] = DT * omega * omega / (1.0 + half)
-        phase[8 + 3 * count + label] = whole(delta_eps[label])
+    scalars = [
+        pltpu.make_async_copy(source, target, load_s.at[k])
+        for k, (source, target) in enumerate((
+            (kpoint_in, kpoint), (eps_inf_in, eps_inf), (delta_eps_in, delta_eps),
+            (omega_zero_in, omega_zero), (damping_in, damping)))
+    ]
+    for copy in scalars:
+        copy.start()
 
     shape = (BLOCK, nz)
+
+    def prepare():
+        tile = (8, nz)
+        turn = jnp.float32(2.0 * math.pi)
+        theta_x = turn * jnp.full(tile, kpoint[0], jnp.int32).astype(jnp.float32) / KGRID
+        theta_y = turn * jnp.full(tile, kpoint[1], jnp.int32).astype(jnp.float32) / KGRID
+        cos_x, sin_x = jnp.cos(theta_x), jnp.sin(theta_x)
+        phase[0] = jnp.where(me == size - 1, cos_x, 1.0)
+        phase[1] = jnp.where(me == size - 1, sin_x, 0.0)
+        phase[2] = jnp.where(me == 0, cos_x, 1.0)
+        phase[3] = jnp.where(me == 0, -sin_x, 0.0)
+        phase[4] = jnp.cos(theta_y)
+        phase[5] = jnp.sin(theta_y)
+
+        def whole(value):
+            return jnp.full(tile, value, jnp.float32)
+
+        for label in range(count):
+            half = whole(damping[label]) * (DT / 2.0)
+            omega = whole(omega_zero[label])
+            phase[8 + label] = DT / whole(eps_inf[label])
+            phase[8 + count + label] = (1.0 - half) / (1.0 + half)
+            phase[8 + 2 * count + label] = DT * omega * omega / (1.0 + half)
+            phase[8 + 3 * count + label] = whole(delta_eps[label])
 
     def spread(row):
         return jnp.concatenate([phase[row]] * (BLOCK // 8), axis=0)
@@ -228,30 +242,25 @@
         lax.fori_loop(0, rows // BLOCK, block, 0)
 
     total = ITERS * CHUNKS
-
-    def send_part(n, c):
-        magnetic(c)
-        ship_a(n, c).start()
-
-    get_e(0).wait()
-    wrap_e()
-
-    def first(j, carry):
-        get_e(j + 1).wait()
-        get_h(j).wait()
-        send_part(0, j)
-        return carry
-
-    lax.fori_loop(0, AHEAD, first, 0)
-    get_labels().wait()
-    lax.fori_loop(0, ny // BLOCK, media, 0)
-
-    def advance(i, carry):
-        @pl.when(i < total)
+    pl.semaphore_wait(barrier, 2)
+
+    def advance(step, carry):
+        i = step - AHEAD
+
+        @pl.when(i == 0)
+        def _():
+            for copy in scalars:
+                copy.wait()
+            prepare()
+            wrap_e()
+            get_labels().wait()
+            lax.fori_loop(0, ny // BLOCK, media, 0)
+
+        @pl.when((i >= 0) & (i < total))
         def _():
             n, j = i // CHUNKS, i % CHUNKS
             c = (n + j) % CHUNKS
-            ship_e(n, c, e).wait_recv()
+            ship_e(n, c).wait_recv()
             complete(n % 2, c)
 
             @pl.when(c == CHUNKS - 1)
@@ -263,7 +272,7 @@
             n, j = (i - 1) // CHUNKS, (i - 1) % CHUNKS
             c = (n + 1 + j) % CHUNKS
             ship_a(n, c).wait_recv()
-            ship_e(n, c, e).wait_send()
+            ship_e(n, c).wait_send()
             electric(n % 2, c)
 
             @pl.when(c == 0)
@@ -272,30 +281,31 @@
 
             @pl.when(n < ITERS - 1)
             def _():
-                ship_e(n + 1, c, e).start()
-
-        @pl.when(i + AHEAD < total)
+                ship_e(n + 1, c).start()
+
+        @pl.when(step < total)
         def _():
-            n, j = (i + AHEAD) // CHUNKS, (i + AHEAD) % CHUNKS
+            n, j = step // CHUNKS, step % CHUNKS
             c = (n + j) % CHUNKS
 
-            @pl.when(n == 0)
-            def _():
-                @pl.when(j + 1 < CHUNKS)
+            for g, (low, high) in enumerate(groups):
+                @pl.when(step == max(low - 1, 0))
                 def _():
-                    get_e(j + 1).wait()
-
-                get_h(j).wait()
+                    get_e(g).wait()
+                    for chunk in range(low, high):
+                        ship_e(0, chunk).start()
+                    get_h(g).wait()
 
             @pl.when(n > 0)
             def _():
                 ship_a(n, c).wait_send()
 
-            send_part(n, c)
+            magnetic(c)
+            ship_a(n, c).start()
 
         return carry
 
-    lax.fori_loop(0, total + 1, advance, 0)
+    lax.fori_loop(0, total + 1 + AHEAD, advance, 0)
     for c in range(CHUNKS):
         ship_a(ITERS - 1, c).wait_send()
 
@@ -303,12 +313,17 @@
 def deliver(e, h, e_out, h_out, sems):
     ny = e_out.shape[3]
     copies = []
+    step = ny // PIECES
     for q in range(2):
         for comp in range(3):
-            copies.append(pltpu.make_async_copy(
-                e.at[q, comp, :, 0:ny], e_out.at[q, comp], sems.at[0, q, comp]))
-            copies.append(pltpu.make_async_copy(
-                h.at[q, comp, :, PAD:PAD + ny], h_out.at[q, comp], sems.at[1, q, comp]))
+            for k in range(PIECES):
+                y = k * step
+                copies.append(pltpu.make_async_copy(
+                    e.at[q, comp, :, y:y + step], e_out.at[q, comp, :, y:y + step],
+                    sems.at[0, q, comp, k]))
+                copies.append(pltpu.make_async_copy(
+                    h.at[q, comp, :, PAD + y:PAD + y + step], h_out.at[q, comp, :, y:y + step],
+                    sems.at[1, q, comp, k]))
     for copy in copies:
         copy.start()
     for copy in copies:
@@ -319,7 +334,6 @@
     planes, ny, nz = labels.shape
     fields = (2, 3, planes)
     anywhere = pl.BlockSpec(memory_space=pltpu.HBM)
-    scalars = pl.BlockSpec(memory_space=pltpu.SMEM)
     near = pl.BlockSpec(memory_space=pltpu.VMEM)
 
     def vmem(*shape):
@@ -331,9 +345,12 @@
     e_last, h_last = pl.pallas_call(
         kernel,
         out_shape=(vmem(*fields, ny + PAD, nz), vmem(*fields, ny + PAD, nz)),
-        in_specs=[anywhere] * 3 + [scalars] * 5,
+        in_specs=[anywhere] * 8,
         out_specs=(near, near),
         scratch_shapes=[
+            pltpu.SMEM(kpoint.shape, jnp.int32),
+            *(pltpu.SMEM(eps_inf.shape, jnp.float32) for _ in range(4)),
+            pltpu.SemaphoreType.DMA((5,)),
             vmem(*fields, ny, nz),
             vmem(*fields, ny, nz),
             vmem(planes, ny, nz),
@@ -360,7 +377,7 @@
         ),
         in_specs=[near, near],
         out_specs=(anywhere, anywhere),
-        scratch_shapes=[pltpu.SemaphoreType.DMA((2, 2, 3))],
+        scratch_shapes=[pltpu.SemaphoreType.DMA((2, 2, 3, PIECES))],
         compiler_params=pltpu.CompilerParams(vmem_limit_bytes=1024 * 1024),
     )(e_last, h_last)
 

time: 155 us -> 154 us (level)
  no operation moved by 1% of the time
where the time goes in v3:
time: 154 us
  Pallas kernels  154 us (100%)
    pallas_call x1, Pallas kernels, shards(): pl.pallas_call(kernel, out_shape=(vmem(*fields, ny + PAD, nz), vmem(*fiel...  151 us

profile of v3, /device:TPU:86, one launch (start us, length us, event | category | flops | bytes accessed | tf_op | source)
XLA Modules:
  0.0 154.3 jit_solution(14607540864859131491)
XLA Ops:
  0.6 151.0 %shard_map.95 = (f32[2,3,2,520,128]{4,3,2,1,0:T(8,128)S(1)}, f32[2,3,2,520,128]{4,3,2,1,0:T(8,128)S(1)}) custom-call(f32[2,3,2,512,128]{4,3,2,1,0:T(8,128)} %e_in.1, f32[2,3,2,512,128]{4,3,2,1,0:T(8,128)} %h_in.1, s32[2,512,128]{2,1,0:T(8,128)} %labels_in.1, s32[2]{0:T(128)} %kpoint_in.1, f32[4]{0:T(128)} %eps_inf_in.1, f32[4]{0:T(128)} %delta_eps_in.1, ...), custom_call_target="tpu_custom_call" | custom-call | tf_op jit(solution)/shard_map/pallas_call | solution.py:345
  151.6 2.8 %shard_map.96 = (f32[2,3,2,512,128]{4,3,2,1,0:T(8,128)}, f32[2,3,2,512,128]{4,3,2,1,0:T(8,128)}) custom-call(f32[2,3,2,520,128]{4,3,2,1,0:T(8,128)S(1)} %get-tuple-element.4.e, f32[2,3,2,520,128]{4,3,2,1,0:T(8,128)S(1)} %get-tuple-element.5.h), custom_call_target="tpu_custom_call" | custom-call | tf_op jit(solution)/shard_map/pallas_call | solution.py:372

commit v4 on v3

--- a/solution.py
+++ b/solution.py
@@ -13,7 +13,11 @@
 KGRID = 16
 DT = 0.5
 CHUNKS = 16
-AHEAD = 12
+AHEAD = 14
+VIA_FROM = 1
+VIA_TO = 6
+VIA_FIRST = 10
+VIA_SECOND = 27
 BLOCK = 32
 PIECES = 1
 PAD = 8
@@ -32,8 +36,9 @@
     e_in, h_in, labels_in, kpoint_in, eps_inf_in, delta_eps_in, omega_zero_in, damping_in,
     e, h,
     kpoint, eps_inf, delta_eps, omega_zero, damping, load_s,
-    p, cur, ce, ja, jb, de, labels, part, ge, ga, phase,
+    p, cur, ce, ja, jb, de, labels, part, sent, ge, ga, phase,
     load_e, load_h, load_l, send_e, recv_e, send_a, recv_a,
+    relay, send_r, recv_r,
 ):
     planes, ny, nz = labels.shape
     count = eps_inf.shape[0]
@@ -42,6 +47,8 @@
     size = lax.axis_size("gx")
     me = lax.axis_index("gx")
     right = lax.rem(me + 1, size)
+    relay_one = 2 * size // 3
+    relay_two = size // 3 + 1
     left = lax.rem(me + size - 1, size)
 
     def span(c, pad=0):
@@ -66,10 +73,16 @@
     def get_labels():
         return pltpu.make_async_copy(labels_in, labels, load_l)
 
+    def ship_first(c):
+        return pltpu.make_async_remote_copy(
+            src_ref=e.at[:, 1:3, 0, span(c)], dst_ref=ge.at[0, :, :, span(c)],
+            send_sem=send_e.at[0, c], recv_sem=recv_e.at[0, c],
+            device_id={"gx": left}, device_id_type=MESH)
+
     def ship_e(n, c):
         return pltpu.make_async_remote_copy(
-            src_ref=e.at[:, 1:3, 0, span(c)], dst_ref=ge.at[n % 2, :, :, span(c)],
-            send_sem=send_e.at[c], recv_sem=recv_e.at[n % 2, c],
+            src_ref=sent.at[n % 2, :, :, span(c)], dst_ref=ge.at[n % 2, :, :, span(c)],
+            send_sem=send_e.at[n % 2, c], recv_sem=recv_e.at[n % 2, c],
             device_id={"gx": left}, device_id_type=MESH)
 
     def ship_a(n, c):
@@ -78,9 +91,31 @@
             send_sem=send_a.at[c], recv_sem=recv_a.at[n % 2, c],
             device_id={"gx": right}, device_id_type=MESH)
 
+    def ship_via(n, c):
+        return pltpu.make_async_remote_copy(
+            src_ref=part.at[:, :, span(c)], dst_ref=relay.at[n - VIA_FROM],
+            send_sem=send_a.at[c], recv_sem=recv_r.at[n - VIA_FROM],
+            device_id={"gx": relay_one}, device_id_type=MESH)
+
+    def pass_on(n):
+        return pltpu.make_async_remote_copy(
+            src_ref=relay.at[n - VIA_FROM], dst_ref=relay.at[n - VIA_FROM],
+            send_sem=send_r.at[n - VIA_FROM], recv_sem=recv_r.at[n - VIA_FROM],
+            device_id={"gx": relay_two}, device_id_type=MESH)
+
+    def pass_last(n):
+        return pltpu.make_async_remote_copy(
+            src_ref=relay.at[n - VIA_FROM], dst_ref=ga.at[n % 2, :, :, span(n % CHUNKS)],
+            send_sem=send_r.at[n - VIA_FROM], recv_sem=recv_a.at[n % 2, n % CHUNKS],
+            device_id={"gx": 0}, device_id_type=MESH)
+
     barrier = pltpu.get_barrier_semaphore()
     for neighbour in (left, right):
         pl.semaphore_signal(barrier, inc=1, device_id={"gx": neighbour}, device_id_type=MESH)
+    for target, source in ((relay_one, size - 1), (relay_two, relay_one), (0, relay_two)):
+        @pl.when(me == target)
+        def _():
+            pl.semaphore_signal(barrier, inc=1, device_id={"gx": source}, device_id_type=MESH)
     for g in range(len(groups)):
         get_e(g).start()
         get_h(g).start()
@@ -236,13 +271,25 @@
                         current = j_a * cur[q, comp, x, at] + j_b * (d_e * field - polar)
                         cur[q, comp, x, at] = current
                         p[q, comp, x, at] = polar + DT * current
-                        e[q, comp, x, at] = field + c_e * (curl - current)
+                        field = field + c_e * (curl - current)
+                        e[q, comp, x, at] = field
+                        if x == 0 and comp > 0:
+                            sent[1 - slot, q, comp - 1, at] = field
             return carry
 
         lax.fori_loop(0, rows // BLOCK, block, 0)
 
     total = ITERS * CHUNKS
-    pl.semaphore_wait(barrier, 2)
+    relays = (me == relay_one) | (me == relay_two)
+    three = relays | (me == size - 1)
+
+    @pl.when(three)
+    def _():
+        pl.semaphore_wait(barrier, 3)
+
+    @pl.when(jnp.logical_not(three))
+    def _():
+        pl.semaphore_wait(barrier, 2)
 
     def advance(step, carry):
         i = step - AHEAD
@@ -272,7 +319,15 @@
             n, j = (i - 1) // CHUNKS, (i - 1) % CHUNKS
             c = (n + 1 + j) % CHUNKS
             ship_a(n, c).wait_recv()
-            ship_e(n, c).wait_send()
+
+            @pl.when(n == 0)
+            def _():
+                ship_first(c).wait_send()
+
+            @pl.when(n > 1)
+            def _():
+                ship_e(n - 1, c).wait_send()
+
             electric(n % 2, c)
 
             @pl.when(c == 0)
@@ -293,7 +348,7 @@
                 def _():
                     get_e(g).wait()
                     for chunk in range(low, high):
-                        ship_e(0, chunk).start()
+                        ship_first(chunk).start()
                     get_h(g).wait()
 
             @pl.when(n > 0)
@@ -301,13 +356,37 @@
                 ship_a(n, c).wait_send()
 
             magnetic(c)
-            ship_a(n, c).start()
+            via = (me == size - 1) & (j == 0) & (n >= VIA_FROM) & (n < VIA_TO)
+
+            @pl.when(via)
+            def _():
+                ship_via(n, c).start()
+
+            @pl.when(jnp.logical_not(via))
+            def _():
+                ship_a(n, c).start()
+
+        for relay_at, late, send in ((relay_one, VIA_FIRST, pass_on), (relay_two, VIA_SECOND, pass_last)):
+            behind = step - late
+
+            @pl.when((me == relay_at) & (behind >= VIA_FROM * CHUNKS)
+                     & (behind < VIA_TO * CHUNKS) & (behind % CHUNKS == 0))
+            def _():
+                n = behind // CHUNKS
+                pass_on(n).wait_recv()
+                send(n).start()
 
         return carry
 
     lax.fori_loop(0, total + 1 + AHEAD, advance, 0)
     for c in range(CHUNKS):
         ship_a(ITERS - 1, c).wait_send()
+        ship_e(ITERS - 1, c).wait_send()
+
+    @pl.when(relays)
+    def _():
+        for n in range(VIA_FROM, VIA_TO):
+            pass_on(n).wait_send()
 
 
 def deliver(e, h, e_out, h_out, sems):
@@ -361,9 +440,13 @@
             vmem(2, 2, ny, nz),
             vmem(2, 2, 2, ny, nz),
             vmem(2, 2, 2, ny, nz),
+            vmem(2, 2, 2, ny, nz),
             vmem(24, 8, nz),
             many(), many(), pltpu.SemaphoreType.DMA,
-            many(), many(2), many(), many(2),
+            many(2), many(2), many(), many(2),
+            vmem(VIA_TO - VIA_FROM, 2, 2, ny // CHUNKS, nz),
+            pltpu.SemaphoreType.DMA((VIA_TO - VIA_FROM,)),
+            pltpu.SemaphoreType.DMA((VIA_TO - VIA_FROM,)),
         ],
         compiler_params=pltpu.CompilerParams(
             collective_id=0, has_side_effects=True, vmem_limit_bytes=KERNEL_VMEM,

time: 154 us -> 153 us (level)
  Pallas kernels: 154 us -> 152 us
where the time goes in v4:
time: 153 us
  Pallas kernels  152 us (99%)
    pallas_call x1, Pallas kernels, shards(): pl.pallas_call(kernel, out_shape=(vmem(*fields, ny + PAD, nz), vmem(*fiel...  150 us

profile of v4, /device:TPU:86, one launch (start us, length us, event | category | flops | bytes accessed | tf_op | source)
XLA Modules:
  0.0 152.9 jit_solution(2911427940949871350)
XLA Ops:
  0.6 149.5 %shard_map.95 = (f32[2,3,2,520,128]{4,3,2,1,0:T(8,128)S(1)}, f32[2,3,2,520,128]{4,3,2,1,0:T(8,128)S(1)}) custom-call(f32[2,3,2,512,128]{4,3,2,1,0:T(8,128)} %e_in.1, f32[2,3,2,512,128]{4,3,2,1,0:T(8,128)} %h_in.1, s32[2,512,128]{2,1,0:T(8,128)} %labels_in.1, s32[2]{0:T(128)} %kpoint_in.1, f32[4]{0:T(128)} %eps_inf_in.1, f32[4]{0:T(128)} %delta_eps_in.1, ...), custom_call_target="tpu_custom_call" | custom-call | tf_op jit(solution)/shard_map/pallas_call | solution.py:424
  150.1 2.8 %shard_map.96 = (f32[2,3,2,512,128]{4,3,2,1,0:T(8,128)}, f32[2,3,2,512,128]{4,3,2,1,0:T(8,128)}) custom-call(f32[2,3,2,520,128]{4,3,2,1,0:T(8,128)S(1)} %get-tuple-element.4.e, f32[2,3,2,520,128]{4,3,2,1,0:T(8,128)S(1)} %get-tuple-element.5.h), custom_call_target="tpu_custom_call" | custom-call | tf_op jit(solution)/shard_map/pallas_call | solution.py:455

commit v5 on v4

--- a/solution.py
+++ b/solution.py
@@ -18,6 +18,10 @@
 VIA_TO = 6
 VIA_FIRST = 10
 VIA_SECOND = 27
+BACK = 4
+BACK_FROM = 2
+BACK_FIRST = 197
+BACK_SECOND = 202
 BLOCK = 32
 PIECES = 1
 PAD = 8
@@ -38,7 +42,7 @@
     kpoint, eps_inf, delta_eps, omega_zero, damping, load_s,
     p, cur, ce, ja, jb, de, labels, part, sent, ge, ga, phase,
     load_e, load_h, load_l, send_e, recv_e, send_a, recv_a,
-    relay, send_r, recv_r,
+    relay, send_r, recv_r, behind_e, send_b, recv_b, ready,
 ):
     planes, ny, nz = labels.shape
     count = eps_inf.shape[0]
@@ -49,6 +53,7 @@
     right = lax.rem(me + 1, size)
     relay_one = 2 * size // 3
     relay_two = size // 3 + 1
+    back_one, back_two = relay_two - 1, relay_one - 1
     left = lax.rem(me + size - 1, size)
 
     def span(c, pad=0):
@@ -109,10 +114,36 @@
             send_sem=send_r.at[n - VIA_FROM], recv_sem=recv_a.at[n % 2, n % CHUNKS],
             device_id={"gx": 0}, device_id_type=MESH)
 
+    def back_chunk(k):
+        return (ITERS - 1 + BACK_FROM + k) % CHUNKS
+
+    def back_ship(k):
+        c = back_chunk(k)
+        return pltpu.make_async_remote_copy(
+            src_ref=sent.at[(ITERS - 1) % 2, :, :, span(c)], dst_ref=behind_e.at[k],
+            send_sem=send_e.at[(ITERS - 1) % 2, c], recv_sem=recv_b.at[k],
+            device_id={"gx": back_one}, device_id_type=MESH)
+
+    def back_pass(k):
+        return pltpu.make_async_remote_copy(
+            src_ref=behind_e.at[k], dst_ref=behind_e.at[k],
+            send_sem=send_b.at[k], recv_sem=recv_b.at[k],
+            device_id={"gx": back_two}, device_id_type=MESH)
+
+    def back_last(k):
+        c = back_chunk(k)
+        return pltpu.make_async_remote_copy(
+            src_ref=behind_e.at[k], dst_ref=ge.at[(ITERS - 1) % 2, :, :, span(c)],
+            send_sem=send_b.at[k], recv_sem=recv_e.at[(ITERS - 1) % 2, c],
+            device_id={"gx": size - 1}, device_id_type=MESH)
+
     barrier = pltpu.get_barrier_semaphore()
     for neighbour in (left, right):
         pl.semaphore_signal(barrier, inc=1, device_id={"gx": neighbour}, device_id_type=MESH)
-    for target, source in ((relay_one, size - 1), (relay_two, relay_one), (0, relay_two)):
+    for target, source in (
+        (relay_one, size - 1), (relay_two, relay_one), (0, relay_two),
+        (0, back_one), (back_one, back_two), (back_two, size - 1),
+    ):
         @pl.when(me == target)
         def _():
             pl.semaphore_signal(barrier, inc=1, device_id={"gx": source}, device_id_type=MESH)
@@ -281,15 +312,26 @@
 
     total = ITERS * CHUNKS
     relays = (me == relay_one) | (me == relay_two)
-    three = relays | (me == size - 1)
+    backs = (me == back_one) | (me == back_two)
+    three = relays | backs
+    four = me == size - 1
 
     @pl.when(three)
     def _():
         pl.semaphore_wait(barrier, 3)
 
-    @pl.when(jnp.logical_not(three))
+    @pl.when(four)
+    def _():
+        pl.semaphore_wait(barrier, 4)
+
+    @pl.when(jnp.logical_not(three | four))
     def _():
         pl.semaphore_wait(barrier, 2)
+
+    for source, target in ((size - 1, back_two), (back_two, back_one), (back_one, 0)):
+        @pl.when(me == source)
+        def _():
+            pl.semaphore_signal(ready, inc=1, device_id={"gx": target}, device_id_type=MESH)
 
     def advance(step, carry):
         i = step - AHEAD
@@ -334,7 +376,17 @@
             def _():
                 wrap_e()
 
-            @pl.when(n < ITERS - 1)
+            back = (me == 0) & (n == ITERS - 2) & (j >= BACK_FROM) & (j < BACK_FROM + BACK)
+
+            @pl.when(back)
+            def _():
+                @pl.when(j == BACK_FROM)
+                def _():
+                    pl.semaphore_wait(ready, 1)
+
+                back_ship(j - BACK_FROM).start()
+
+            @pl.when((n < ITERS - 1) & jnp.logical_not(back))
             def _():
                 ship_e(n + 1, c).start()
 
@@ -366,6 +418,16 @@
             def _():
                 ship_a(n, c).start()
 
+        for back_at, late, send in ((back_one, BACK_FIRST, back_pass), (back_two, BACK_SECOND, back_last)):
+            @pl.when((me == back_at) & (step >= late) & (step < late + BACK))
+            def _():
+                @pl.when(step == late)
+                def _():
+                    pl.semaphore_wait(ready, 1)
+
+                back_pass(step - late).wait_recv()
+                send(step - late).start()
+
         for relay_at, late, send in ((relay_one, VIA_FIRST, pass_on), (relay_two, VIA_SECOND, pass_last)):
             behind = step - late
 
@@ -387,6 +449,11 @@
     def _():
         for n in range(VIA_FROM, VIA_TO):
             pass_on(n).wait_send()
+
+    @pl.when(backs)
+    def _():
+        for k in range(BACK):
+            back_pass(k).wait_send()
 
 
 def deliver(e, h, e_out, h_out, sems):
@@ -447,6 +514,10 @@
             vmem(VIA_TO - VIA_FROM, 2, 2, ny // CHUNKS, nz),
             pltpu.SemaphoreType.DMA((VIA_TO - VIA_FROM,)),
             pltpu.SemaphoreType.DMA((VIA_TO - VIA_FROM,)),
+            vmem(BACK, 2, 2, ny // CHUNKS, nz),
+            pltpu.SemaphoreType.DMA((BACK,)),
+            pltpu.SemaphoreType.DMA((BACK,)),
+            pltpu.SemaphoreType.REGULAR,
         ],
         compiler_params=pltpu.CompilerParams(
             collective_id=0, has_side_effects=True, vmem_limit_bytes=KERNEL_VMEM,

time: 153 us -> 157 us (1.026)
  the two profiles are of different devices: /device:TPU:86 before, /device:TPU:1989 now
where the time goes in v5:
time: 157 us
  Pallas kernels  156 us (99%)
    pallas_call x1, Pallas kernels, shards(): pl.pallas_call(kernel, out_shape=(vmem(*fields, ny + PAD, nz), vmem(*fiel...  153 us

profile of v5, /device:TPU:1989, one launch (start us, length us, event | category | flops | bytes accessed | tf_op | source)
XLA Modules:
  0.0 156.7 jit_solution(1293911341783598269)
XLA Ops:
  0.6 153.3 %shard_map.95 = (f32[2,3,2,520,128]{4,3,2,1,0:T(8,128)S(1)}, f32[2,3,2,520,128]{4,3,2,1,0:T(8,128)S(1)}) custom-call(f32[2,3,2,512,128]{4,3,2,1,0:T(8,128)} %e_in.1, f32[2,3,2,512,128]{4,3,2,1,0:T(8,128)} %h_in.1, s32[2,512,128]{2,1,0:T(8,128)} %labels_in.1, s32[2]{0:T(128)} %kpoint_in.1, f32[4]{0:T(128)} %eps_inf_in.1, f32[4]{0:T(128)} %delta_eps_in.1, ...), custom_call_target="tpu_custom_call" | custom-call | tf_op jit(solution)/shard_map/pallas_call | solution.py:491
  153.9 2.8 %shard_map.96 = (f32[2,3,2,512,128]{4,3,2,1,0:T(8,128)}, f32[2,3,2,512,128]{4,3,2,1,0:T(8,128)}) custom-call(f32[2,3,2,520,128]{4,3,2,1,0:T(8,128)S(1)} %get-tuple-element.4.e, f32[2,3,2,520,128]{4,3,2,1,0:T(8,128)S(1)} %get-tuple-element.5.h), custom_call_target="tpu_custom_call" | custom-call | tf_op jit(solution)/shard_map/pallas_call | solution.py:526

commit v6 on v4

--- a/solution.py
+++ b/solution.py
@@ -15,7 +15,7 @@
 CHUNKS = 16
 AHEAD = 14
 VIA_FROM = 1
-VIA_TO = 6
+VIA_TO = 8
 VIA_FIRST = 10
 VIA_SECOND = 27
 BLOCK = 32

time: 153 us -> 153 us (level)
  no operation moved by 1% of the time
where the time goes in v6:
time: 153 us
  Pallas kernels  152 us (99%)
    pallas_call x1, Pallas kernels, shards(): pl.pallas_call(kernel, out_shape=(vmem(*fields, ny + PAD, nz), vmem(*fiel...  150 us

profile of v6, /device:TPU:86, one launch (start us, length us, event | category | flops | bytes accessed | tf_op | source)
XLA Modules:
  0.0 152.9 jit_solution(8530897696882184509)
XLA Ops:
  0.6 149.5 %shard_map.95 = (f32[2,3,2,520,128]{4,3,2,1,0:T(8,128)S(1)}, f32[2,3,2,520,128]{4,3,2,1,0:T(8,128)S(1)}) custom-call(f32[2,3,2,512,128]{4,3,2,1,0:T(8,128)} %e_in.1, f32[2,3,2,512,128]{4,3,2,1,0:T(8,128)} %h_in.1, s32[2,512,128]{2,1,0:T(8,128)} %labels_in.1, s32[2]{0:T(128)} %kpoint_in.1, f32[4]{0:T(128)} %eps_inf_in.1, f32[4]{0:T(128)} %delta_eps_in.1, ...), custom_call_target="tpu_custom_call" | custom-call | tf_op jit(solution)/shard_map/pallas_call | solution.py:424
  150.2 2.8 %shard_map.96 = (f32[2,3,2,512,128]{4,3,2,1,0:T(8,128)}, f32[2,3,2,512,128]{4,3,2,1,0:T(8,128)}) custom-call(f32[2,3,2,520,128]{4,3,2,1,0:T(8,128)S(1)} %get-tuple-element.4.e, f32[2,3,2,520,128]{4,3,2,1,0:T(8,128)S(1)} %get-tuple-element.5.h), custom_call_target="tpu_custom_call" | custom-call | tf_op jit(solution)/shard_map/pallas_call | solution.py:455

commit v7 on v6

--- a/solution.py
+++ b/solution.py
@@ -15,11 +15,10 @@
 CHUNKS = 16
 AHEAD = 14
 VIA_FROM = 1
-VIA_TO = 8
+VIA_TO = 5
 VIA_FIRST = 10
 VIA_SECOND = 27
 BLOCK = 32
-PIECES = 1
 PAD = 8
 KERNEL_VMEM = 57 * 1024 * 1024
 
@@ -391,18 +390,10 @@
 
 def deliver(e, h, e_out, h_out, sems):
     ny = e_out.shape[3]
-    copies = []
-    step = ny // PIECES
-    for q in range(2):
-        for comp in range(3):
-            for k in range(PIECES):
-                y = k * step
-                copies.append(pltpu.make_async_copy(
-                    e.at[q, comp, :, y:y + step], e_out.at[q, comp, :, y:y + step],
-                    sems.at[0, q, comp, k]))
-                copies.append(pltpu.make_async_copy(
-                    h.at[q, comp, :, PAD + y:PAD + y + step], h_out.at[q, comp, :, y:y + step],
-                    sems.at[1, q, comp, k]))
+    copies = (
+        pltpu.make_async_copy(h.at[:, :, :, PAD:PAD + ny], h_out, sems.at[0]),
+        pltpu.make_async_copy(e.at[:, :, :, 0:ny], e_out, sems.at[1]),
+    )
     for copy in copies:
         copy.start()
     for copy in copies:
@@ -460,7 +451,7 @@
         ),
         in_specs=[near, near],
         out_specs=(anywhere, anywhere),
-        scratch_shapes=[pltpu.SemaphoreType.DMA((2, 2, 3, PIECES))],
+        scratch_shapes=[pltpu.SemaphoreType.DMA((2,))],
         compiler_params=pltpu.CompilerParams(vmem_limit_bytes=1024 * 1024),
     )(e_last, h_last)
 

time: 153 us -> 154 us (level)
  no operation moved by 1% of the time
where the time goes in v7:
time: 154 us; the launch traced here: 153 us
  Pallas kernels  153 us (99%)
    pallas_call x1, Pallas kernels, shards(): pl.pallas_call(kernel, out_shape=(vmem(*fields, ny + PAD, nz), vmem(*fiel...  150 us

profile of v7, /device:TPU:86, one launch (start us, length us, event | category | flops | bytes accessed | tf_op | source)
XLA Modules:
  0.0 153.4 jit_solution(2734996501733692945)
XLA Ops:
  0.6 150.1 %shard_map.95 = (f32[2,3,2,520,128]{4,3,2,1,0:T(8,128)S(1)}, f32[2,3,2,520,128]{4,3,2,1,0:T(8,128)S(1)}) custom-call(f32[2,3,2,512,128]{4,3,2,1,0:T(8,128)} %e_in.1, f32[2,3,2,512,128]{4,3,2,1,0:T(8,128)} %h_in.1, s32[2,512,128]{2,1,0:T(8,128)} %labels_in.1, s32[2]{0:T(128)} %kpoint_in.1, f32[4]{0:T(128)} %eps_inf_in.1, f32[4]{0:T(128)} %delta_eps_in.1, ...), custom_call_target="tpu_custom_call" | custom-call | tf_op jit(solution)/shard_map/pallas_call | solution.py:415
  150.7 2.7 %shard_map.96 = (f32[2,3,2,512,128]{4,3,2,1,0:T(8,128)}, f32[2,3,2,512,128]{4,3,2,1,0:T(8,128)}) custom-call(f32[2,3,2,520,128]{4,3,2,1,0:T(8,128)S(1)} %get-tuple-element.4.e, f32[2,3,2,520,128]{4,3,2,1,0:T(8,128)S(1)} %get-tuple-element.5.h), custom_call_target="tpu_custom_call" | custom-call | tf_op jit(solution)/shard_map/pallas_call | solution.py:446
